TPU v7x, 8 devices: a whole 2x2x1 slice. The times are simulated.
8 devices in a mesh: rep: 1 (over z), dp: 8 (over x, y, core).
Axes of the slice: x: 2, y: 2, z: 1, core: 2. Of those that a mesh axis runs over, the one named last changes fastest.
Arguments:
- x: bfloat16 [8, 2048, 1024], P(('rep', 'dp'))
- dy: bfloat16 [8, 2048, 1024], P(('rep', 'dp'))
- w_gate: bfloat16 [2, 1024, 2816], P(None, 'dp')
- w_up: bfloat16 [2, 1024, 2816], P(None, 'dp')
- w_down: bfloat16 [2, 2816, 1024], P(None, 'dp')
Outputs:
- output 1: bfloat16 [8, 2048, 1024], P(('rep', 'dp'))
- output 2: bfloat16 [2, 1024, 2816], P('rep', 'dp')
- output 3: bfloat16 [2, 1024, 2816], P('rep', 'dp')
- output 4: bfloat16 [2, 2816, 1024], P('rep', 'dp')
All inputs are finite; a program needn't handle non-finite values.
Results may differ from a plain program's by a relative error of at most 0.018.
Values are sent between devices in bfloat16 or wider.
A program may use at most 2 GiB of HBM per device.

v0:
```python
import jax
import jax.numpy as jnp
from jax import lax

NAMES = ("w_gate", "w_up", "w_down")


def matmul(a, w):
    return jnp.dot(a, w, preferred_element_type=jnp.float32).astype(jnp.bfloat16)


def normed(h):
    wide = h.astype(jnp.float32)
    scale = lax.rsqrt(jnp.mean(wide**2, -1, keepdims=True) + 1e-6)
    return (wide * scale).astype(jnp.bfloat16)


def layer(h, w):
    a = normed(h)
    gate = jnp.dot(a, w["w_gate"], preferred_element_type=jnp.float32)
    up = jnp.dot(a, w["w_up"], preferred_element_type=jnp.float32)
    return h + matmul((jax.nn.silu(gate) * up).astype(jnp.bfloat16), w["w_down"])


def stack(weights, h):
    for number in range(weights["w_gate"].shape[0]):
        h = layer(h, {name: w[number] for name, w in weights.items()})
    return h


def solution(mesh):
    groups = mesh.shape["rep"]

    def step(x, dy, *weights):
        shape = x.shape
        x, dy = (t.reshape(groups, -1, *t.shape[1:]) for t in (x, dy))

        def of_a_group(x, dy):
            _, back = jax.vjp(stack, dict(zip(NAMES, weights, strict=True)), x)
            by_weights, by_x = back(dy)
            return (by_x, *(by_weights[name] for name in NAMES))

        by_x, *by_weights = jax.vmap(of_a_group)(x, dy)
        return (by_x.reshape(shape), *(t.reshape(-1, *t.shape[2:]) for t in by_weights))

    return step
```

profile of v0, /device:TPU:0, one launch (start us, length us, event | category | flops | bytes accessed | tf_op | source)
XLA Modules:
  0.0 792.9 jit_solution(4412551036822112709)
XLA Ops:
  7.2 0.0 all-gather.30.cloned.1.call-start
  7.2 2.5 fusion.91
  9.8 0.0 all-gather.32.cloned.1.call-start
  9.8 2.5 fusion.90
  12.4 0.0 all-gather.34.cloned.1.call-start
  12.4 2.5 fusion.92
  15.0 0.0 all-gather.38.cloned.1.call-start
  15.0 0.5 all-gather.38.cloned.1.call-update
  15.6 0.5 all-gather.36.cloned.1.call-update
  16.2 0.5 all-gather.40.cloned.1.call-update
  16.7 0.0 reduce-scatter.23.cloned.1.call-start
  16.8 6.5 copy.1
  23.3 3.1 fusion.36
  26.4 0.6 copy-done.9
  27.0 6.4 copy.2
  33.4 16.7 %all-gather.30.cloned.1.call-done = bf16[1,1024,2816]{2,1,0:T(8,128)(2,1)} async-done(((bf16[1,128,2816]{2,1,0:T(8,128)(2,1)}), bf16[1,1024,2816]{2,1,0:T(8,128)(2,1)}) %all-gather.30.cloned.1.call-update) | async-done | bytes 5767184 | tf_op jit(solution)/vmap(jvp())/squeeze | solution.py:27
  50.1 20.0 %fusion.58 = f32[2048,2816]{1,0:T(8,128)} fusion(bf16[1,1024,2816]{2,1,0:T(8,128)(2,1)} %all-gather.30.cloned.1.call-done, bf16[1,2048,1024]{1,2,0:T(8,128)(2,1)} %copy.1, f32[2048]{0:T(1024)S(1)} %bitcast.243), kind=kOutput, calls=%fused_computation.79 | convolution fusion | flops 11817451520 | bytes 33038336 | tf_op jit(solution)/vmap(jvp())/dot_general | solution.py:20
  70.1 19.8 %all-gather.32.cloned.1.call-done = bf16[1,1024,2816]{2,1,0:T(8,128)(2,1)} async-done(((bf16[1,128,2816]{2,1,0:T(8,128)(2,1)}), bf16[1,1024,2816]{2,1,0:T(8,128)(2,1)}) %all-gather.32.cloned.1.call-update) | async-done | bytes 5767184 | tf_op jit(solution)/vmap(jvp())/squeeze | solution.py:27
  89.9 20.0 %fusion.54 = f32[2048,2816]{1,0:T(8,128)} fusion(bf16[1,1024,2816]{2,1,0:T(8,128)(2,1)} %all-gather.32.cloned.1.call-done, bf16[1,2048,1024]{1,2,0:T(8,128)(2,1)} %copy.1, f32[2048]{0:T(1024)S(1)} %bitcast.244), kind=kOutput, calls=%fused_computation.75 | convolution fusion | flops 11817451520 | bytes 33038336 | tf_op jit(solution)/vmap(jvp())/dot_general | solution.py:21
  109.9 19.7 %fusion.24 = bf16[2048,2816]{1,0:T(8,128)(2,1)} fusion(f32[2048,2816]{1,0:T(8,128)} %fusion.54, f32[2048,2816]{1,0:T(8,128)} %fusion.58), kind=kLoop, calls=%fused_computation.42 | loop fusion | flops 34603008 | bytes 57671680
  129.6 19.6 %fusion.39 = (f32[2048]{0:T(1024)S(1)}, bf16[1,2048,1024]{1,2,0:T(8,128)(2,1)}) fusion(bf16[1,2048,1024]{1,2,0:T(8,128)(2,1)} %copy.1, bf16[2048,2816]{1,0:T(8,128)(2,1)} %fusion.24, bf16[1,2816,1024]{2,1,0:T(8,128)(2,1)} %all-gather.34.cloned.1.call-done), kind=kOutput, calls=%fused_computation.60 | convolution fusion | flops 11821643776 | bytes 25698304 | tf_op jit(solution)/vmap(jvp())/dot_general | solution.py:9
  149.2 0.6 copy-done.11
  149.8 18.3 %all-gather.38.cloned.1.call-done = bf16[1,2816,1024]{2,1,0:T(8,128)(2,1)} async-done(((bf16[1,352,1024]{2,1,0:T(8,128)(2,1)}), bf16[1,2816,1024]{2,1,0:T(8,128)(2,1)}) %all-gather.38.cloned.1.call-update) | async-done | bytes 5767184 | tf_op jit(solution)/vmap(jvp())/squeeze | solution.py:27
  168.1 18.1 %convolution_convert_fusion.1 = bf16[2048,2816]{1,0:T(8,128)(2,1)} fusion(bf16[1,2816,1024]{2,1,0:T(8,128)(2,1)} %all-gather.38.cloned.1.call-done, bf16[1,2048,1024]{2,1,0:T(8,128)(2,1)} %param), kind=kOutput, calls=%fused_computation.50 | convolution fusion | flops 11816927232 | bytes 21495808 | tf_op jit(solution)/vmap(transpose(jvp()))/dot_general | solution.py:9
  186.2 21.5 %all-gather.36.cloned.1.call-done = bf16[1,1024,2816]{2,1,0:T(8,128)(2,1)} async-done(((bf16[1,128,2816]{2,1,0:T(8,128)(2,1)}), bf16[1,1024,2816]{2,1,0:T(8,128)(2,1)}) %all-gather.36.cloned.1.call-update) | async-done | bytes 5767184 | tf_op jit(solution)/vmap(jvp())/squeeze | solution.py:27
  207.7 20.5 %fusion.48 = f32[2048,2816]{1,0:T(8,128)} fusion(bf16[1,1024,2816]{2,1,0:T(8,128)(2,1)} %all-gather.36.cloned.1.call-done, bf16[1,2048,1024]{1,2,0:T(8,128)(2,1)} %get-tuple-element.11, f32[2048]{0:T(1024)S(1)} %bitcast.248), kind=kOutput, calls=%fused_computation.69 | convolution fusion | flops 11817451520 | bytes 33038336 | tf_op jit(solution)/vmap(jvp())/dot_general | solution.py:20
  228.2 21.9 %fusion.20 = f32[2816,1024]{1,0:T(8,128)} fusion(bf16[2048,2816]{1,0:T(8,128)(2,1)} %convolution_convert_fusion.1, f32[2048,2816]{1,0:T(8,128)} %fusion.48, bf16[1,2048,1024]{1,2,0:T(8,128)(2,1)S(1)} %copy-done.7, f32[2048]{0:T(1024)S(1)} %bitcast.249), kind=kOutput, calls=%fused_computation.32 | convolution fusion | flops 11852054528 | bytes 50339840 | tf_op jit(solution)/vmap(transpose(jvp()))/dot_general | solution.py:21
  250.1 0.0 reduce-scatter.25.cloned.1.call-start
  250.2 20.1 %fusion.42 = f32[2048,2816]{1,0:T(8,128)} fusion(bf16[1,1024,2816]{2,1,0:T(8,128)(2,1)} %all-gather.40.cloned.1.call-done, bf16[1,2048,1024]{1,2,0:T(8,128)(2,1)} %get-tuple-element.11, f32[2048]{0:T(1024)S(1)} %bitcast.250), kind=kOutput, calls=%fused_computation.63 | convolution fusion | flops 11817451520 | bytes 33038336 | tf_op jit(solution)/vmap(jvp())/dot_general | solution.py:21
  270.3 23.3 %fusion.4 = bf16[2048,2816]{1,0:T(8,128)(2,1)} fusion(f32[2048,2816]{1,0:T(8,128)} %fusion.48, f32[2048,2816]{1,0:T(8,128)} %fusion.42, bf16[2048,2816]{1,0:T(8,128)(2,1)} %convolution_convert_fusion.1), kind=kLoop, calls=%fused_computation.10 | loop fusion | flops 69206016 | bytes 69206016
  293.6 21.6 %fusion.22 = bf16[2048,1024]{0,1:T(8,128)(2,1)} fusion(bf16[2048,2816]{1,0:T(8,128)(2,1)} %convolution_convert_fusion.1, f32[2048,2816]{1,0:T(8,128)} %fusion.48, bf16[1,1024,2816]{2,1,0:T(8,128)(2,1)} %all-gather.40.cloned.1.call-done), kind=kOutput, calls=%fused_computation.33 | convolution fusion | flops 11845763072 | bytes 44564480 | tf_op jit(solution)/vmap(transpose(jvp()))/dot_general | solution.py:21
  315.3 20.3 %fusion.41 = (f32[2048]{0:T(1024)S(1)}, bf16[2048,1024]{0,1:T(8,128)(2,1)}) fusion(bf16[1,2048,1024]{1,2,0:T(8,128)(2,1)} %get-tuple-element.11, bf16[2048,1024]{0,1:T(8,128)(2,1)} %fusion.22, bf16[2048,2816]{1,0:T(8,128)(2,1)} %fusion.4, bf16[1,1024,2816]{2,1,0:T(8,128)(2,1)} %all-gather.36.cloned.1.call-done), kind=kOutput, calls=%fused_computation.62 | convolution fusion | flops 11821643776 | bytes 29892608 | tf_op jit(solution)/vmap(transpose(jvp()))/dot_general | solution.py:20
  335.6 4.7 fusion.63
  340.3 2.0 copy-done.3
  342.4 17.6 %convolution_convert_fusion = bf16[2048,2816]{1,0:T(8,128)(2,1)} fusion(bf16[1,2816,1024]{2,1,0:T(8,128)(2,1)} %all-gather.34.cloned.1.call-done, bf16[1,2048,1024]{1,2,0:T(8,128)(2,1)S(1)} %fusion.63), kind=kOutput, calls=%fused_computation.49 | convolution fusion | flops 11816927232 | bytes 21495808 | tf_op jit(solution)/vmap(transpose(jvp()))/dot_general | solution.py:9
  360.0 22.0 %fusion.16 = f32[2816,1024]{1,0:T(8,128)} fusion(bf16[2048,2816]{1,0:T(8,128)(2,1)} %convolution_convert_fusion, f32[2048,2816]{1,0:T(8,128)} %fusion.58, bf16[1,2048,1024]{1,2,0:T(8,128)(2,1)S(1)} %copy-done, f32[2048]{0:T(1024)S(1)} %bitcast.245), kind=kOutput, calls=%fused_computation.30 | convolution fusion | flops 11852054528 | bytes 50339840 | tf_op jit(solution)/vmap(transpose(jvp()))/dot_general | solution.py:21
  381.9 0.0 reduce-scatter.19.cloned.1.call-start
  382.0 19.3 %fusion.81 = f32[2816,1024]{1,0:T(8,128)} fusion(bf16[2048,2816]{1,0:T(8,128)(2,1)} %fusion.4, bf16[1,2048,1024]{1,2,0:T(8,128)(2,1)} %get-tuple-element.11, f32[2048]{0:T(1024)S(1)} %bitcast.252), kind=kOutput, calls=%fused_computation.94 | convolution fusion | flops 11817451520 | bytes 27271168 | tf_op jit(solution)/vmap(transpose(jvp()))/dot_general | solution.py:20
  401.3 0.0 reduce-scatter.21.cloned.1.call-start
  401.4 19.7 %fusion.7 = bf16[2048,2816]{1,0:T(8,128)(2,1)S(1)} fusion(f32[2048,2816]{1,0:T(8,128)} %fusion.58, f32[2048,2816]{1,0:T(8,128)} %fusion.54, bf16[2048,2816]{1,0:T(8,128)(2,1)} %convolution_convert_fusion), kind=kLoop, calls=%fused_computation.13 | loop fusion | flops 69206016 | bytes 69206016
  421.1 4.3 copy-done.6
  425.4 15.5 %fusion.76 = f32[2816,1024]{1,0:T(8,128)} fusion(bf16[2048,2816]{1,0:T(8,128)(2,1)S(1)} %fusion.7, bf16[1,2048,1024]{1,2,0:T(8,128)(2,1)S(1)} %copy-done.1, f32[2048]{0:T(1024)S(1)} %bitcast.246), kind=kOutput, calls=%fused_computation.93 | convolution fusion | flops 11817451520 | bytes 27271168 | tf_op jit(solution)/vmap(transpose(jvp()))/dot_general | solution.py:20
  440.9 0.0 reduce-scatter.27.cloned.1.call-start
  440.9 25.6 %fusion.26 = f32[2816,1024]{1,0:T(8,128)} fusion(f32[2048,2816]{1,0:T(8,128)} %fusion.42, f32[2048,2816]{1,0:T(8,128)} %fusion.48, bf16[1,2048,1024]{2,1,0:T(8,128)(2,1)} %param), kind=kOutput, calls=%fused_computation.44 | convolution fusion | flops 11845763072 | bytes 61865984 | tf_op jit(solution)/vmap(transpose(jvp()))/dot_general | solution.py:9
  466.5 0.0 reduce-scatter.29.cloned.1.call-start
  466.6 18.8 %fusion.64 = f32[1024,2816]{0,1:T(8,128)} fusion(bf16[2048,2816]{1,0:T(8,128)(2,1)} %fusion.24, bf16[1,2048,1024]{1,2,0:T(8,128)(2,1)} %copy-done.3), kind=kOutput, calls=%fused_computation.85 | convolution fusion | flops 11811160064 | bytes 27262976 | tf_op jit(solution)/vmap(transpose(jvp()))/dot_general | solution.py:9
  485.3 22.0 %fusion.18 = bf16[2048,1024]{0,1:T(8,128)(2,1)} fusion(bf16[2048,2816]{1,0:T(8,128)(2,1)} %convolution_convert_fusion, f32[2048,2816]{1,0:T(8,128)} %fusion.58, bf16[1,1024,2816]{2,1,0:T(8,128)(2,1)} %all-gather.32.cloned.1.call-done), kind=kOutput, calls=%fused_computation.31 | convolution fusion | flops 11845763072 | bytes 44564480 | tf_op jit(solution)/vmap(transpose(jvp()))/dot_general | solution.py:21
  507.3 18.9 %fusion.38 = (f32[2048]{0:T(1024)S(1)}, bf16[2048,1024]{0,1:T(8,128)(2,1)S(1)}) fusion(bf16[1,2048,1024]{1,2,0:T(8,128)(2,1)} %copy.1, bf16[2048,1024]{0,1:T(8,128)(2,1)} %fusion.18, bf16[2048,2816]{1,0:T(8,128)(2,1)} %copy-done.6, bf16[1,1024,2816]{2,1,0:T(8,128)(2,1)} %all-gather.30.cloned.1.call-done), kind=kOutput, calls=%fused_computation.59 | convolution fusion | flops 11821643776 | bytes 29892608 | tf_op jit(solution)/vmap(transpose(jvp()))/dot_general | solution.py:20
  526.3 4.7 fusion.62
  531.0 6.4 copy.3
  537.4 1.4 convert_bitcast_fusion.3
  538.8 1.4 convert_bitcast_fusion.2
  540.3 0.1 add_bitcast_fusion.1
  540.4 1.5 copy.5
  541.9 1.4 convert_bitcast_fusion.5
  543.4 77.9 %reduce-scatter.21.cloned.1.call-done = f32[2816,128]{1,0:T(8,128)} async-done(((f32[2816,1024]{1,0:T(8,128)}), f32[2816,128]{1,0:T(8,128)}) %reduce-scatter.21.cloned.1.call-update) | async-done | bytes 1441808
  621.3 1.4 convert_bitcast_fusion.4
  622.7 0.1 add_bitcast_fusion.2
  622.8 1.5 copy.4
  624.4 77.8 %reduce-scatter.27.cloned.1.call-done = f32[352,1024]{1,0:T(8,128)} async-done(((f32[2816,1024]{1,0:T(8,128)}), f32[352,1024]{1,0:T(8,128)}) %reduce-scatter.27.cloned.1.call-update) | async-done | bytes 1441808
  702.2 1.5 convert_bitcast_fusion.1
  703.7 79.3 %reduce-scatter.29.cloned.1.call-done = f32[1024,352]{0,1:T(8,128)} async-done(((f32[1024,2816]{0,1:T(8,128)}), f32[1024,352]{0,1:T(8,128)}) %reduce-scatter.29.cloned.1.call-update) | async-done | bytes 1441808
  783.0 1.5 convert_bitcast_fusion
  784.4 1.2 add_bitcast_fusion
  (50 shorter events, 0.4 us)
Async XLA Ops:
  7.2 42.9 %all-gather.30.cloned.1.call-start = ((), (), s32[]{:S(2)}) async-start(), calls=%async_computation.6 | async-start | bytes 6488064 | tf_op jit(solution)/vmap(jvp())/squeeze | solution.py:27
  9.8 80.1 %all-gather.32.cloned.1.call-start = ((), (), s32[]{:S(2)}) async-start(), calls=%async_computation.7 | async-start | bytes 6488064 | tf_op jit(solution)/vmap(jvp())/squeeze | solution.py:27
  12.4 117.2 %all-gather.34.cloned.1.call-start = ((), (), s32[]{:S(2)}) async-start(), calls=%async_computation.8 | async-start | bytes 6488064 | tf_op jit(solution)/vmap(jvp())/squeeze | solution.py:27
  15.0 153.1 %all-gather.38.cloned.1.call-start = ((), (), s32[]{:S(2)}) async-start(), calls=%async_computation.10 | async-start | bytes 6488064 | tf_op jit(solution)/vmap(jvp())/squeeze | solution.py:27
  15.6 192.1 %all-gather.36.cloned.1.call-start = ((), (), s32[]{:S(2)}) async-start(), calls=%async_computation.9 | async-start | bytes 6488064 | tf_op jit(solution)/vmap(jvp())/squeeze | solution.py:27
  16.2 234.0 %all-gather.40.cloned.1.call-start = ((), (), s32[]{:S(2)}) async-start(), calls=%async_computation.11 | async-start | bytes 6488064 | tf_op jit(solution)/vmap(jvp())/squeeze | solution.py:27
  16.7 520.6 %reduce-scatter.23.cloned.1.call-start = ((), (), s32[]{:S(2)}) async-start(), calls=%async_computation.14 | async-start | bytes 12976128
  26.4 0.6 copy-start.9
  27.0 62.9 %copy-start.13 = (f32[1,2048]{1,0:T(1,128)}, f32[1,2048]{1,0:T(1,128)S(1)}, u32[]{:S(2)}) copy-start(f32[1,2048]{1,0:T(1,128)S(1)} %rsqrt.22) | copy-start | bytes 24580
  149.2 0.6 copy-start.11
  207.7 20.5 %copy-start.7 = (bf16[1,2048,1024]{1,2,0:T(8,128)(2,1)S(1)}, bf16[1,2048,1024]{1,2,0:T(8,128)(2,1)}, u32[]{:S(2)}) copy-start(bf16[1,2048,1024]{1,2,0:T(8,128)(2,1)} %get-tuple-element.11) | copy-start | bytes 12582916
  250.1 288.7 %reduce-scatter.25.cloned.1.call-start = ((), (), s32[]{:S(2)}) async-start(), calls=%async_computation.15 | async-start | bytes 12976128
  315.3 20.3 %copy-start.12 = (f32[2048]{0:T(1024)S(1)}, f32[2048]{0:T(1024)}, u32[]{:S(2)}) copy-start(f32[2048]{0:T(1024)} %copy-done.11) | copy-start | bytes 24580
  315.3 20.3 %copy-start.5 = (bf16[1,2048,1024]{1,2,0:T(8,128)(2,1)S(1)}, bf16[1,2048,1024]{1,2,0:T(8,128)(2,1)}, u32[]{:S(2)}) copy-start(bf16[1,2048,1024]{1,2,0:T(8,128)(2,1)} %copy.2) | copy-start | bytes 12582916
  315.3 20.3 %copy-start.8 = (bf16[1,2048,1024]{1,2,0:T(8,128)(2,1)S(1)}, bf16[1,2048,1024]{1,2,0:T(8,128)(2,1)}, u32[]{:S(2)}) copy-start(bf16[1,2048,1024]{1,2,0:T(8,128)(2,1)} %get-tuple-element.11) | copy-start | bytes 12582916
  340.3 2.0 copy-start.3
  342.4 17.6 %copy-start = (bf16[1,2048,1024]{1,2,0:T(8,128)(2,1)S(1)}, bf16[1,2048,1024]{1,2,0:T(8,128)(2,1)}, u32[]{:S(2)}) copy-start(bf16[1,2048,1024]{1,2,0:T(8,128)(2,1)} %copy.1) | copy-start | bytes 12582916
  342.4 17.6 %copy-start.14 = (f32[1,2048]{1,0:T(1,128)S(1)}, f32[1,2048]{1,0:T(1,128)}, u32[]{:S(2)}) copy-start(f32[1,2048]{1,0:T(1,128)} %copy-done.13) | copy-start | bytes 24580
  381.9 160.0 %reduce-scatter.19.cloned.1.call-start = ((), (), s32[]{:S(2)}) async-start(), calls=%async_computation.12 | async-start | bytes 12976128
  401.3 220.0 %reduce-scatter.21.cloned.1.call-start = ((), (), s32[]{:S(2)}) async-start(), calls=%async_computation.13 | async-start | bytes 12976128
  401.4 24.0 %copy-start.1 = (bf16[1,2048,1024]{1,2,0:T(8,128)(2,1)S(1)}, bf16[1,2048,1024]{1,2,0:T(8,128)(2,1)}, u32[]{:S(2)}) copy-start(bf16[1,2048,1024]{1,2,0:T(8,128)(2,1)} %copy.1) | copy-start | bytes 12582916
  421.0 4.3 copy-start.6
  440.9 261.3 %reduce-scatter.27.cloned.1.call-start = ((), (), s32[]{:S(2)}) async-start(), calls=%async_computation.16 | async-start | bytes 12976128
  466.5 316.5 %reduce-scatter.29.cloned.1.call-start = ((), (), s32[]{:S(2)}) async-start(), calls=%async_computation.17 | async-start | bytes 12976128
  507.3 18.9 %copy-start.10 = (f32[2048]{0:T(1024)S(1)}, f32[2048]{0:T(1024)}, u32[]{:S(2)}) copy-start(f32[2048]{0:T(1024)} %copy-done.9) | copy-start | bytes 24580
  507.3 19.0 %copy-start.2 = (bf16[1,2048,1024]{1,2,0:T(8,128)(2,1)S(1)}, bf16[1,2048,1024]{1,2,0:T(8,128)(2,1)}, u32[]{:S(2)}) copy-start(bf16[1,2048,1024]{1,2,0:T(8,128)(2,1)} %copy.1) | copy-start | bytes 12582916
  507.3 19.0 %copy-start.4 = (bf16[1,2048,1024]{1,2,0:T(8,128)(2,1)S(1)}, bf16[1,2048,1024]{1,2,0:T(8,128)(2,1)}, u32[]{:S(2)}) copy-start(bf16[1,2048,1024]{1,2,0:T(8,128)(2,1)} %copy-done.3) | copy-start | bytes 12582916
  507.3 19.0 %copy-start.15 = (f32[1,2048]{1,0:T(1,128)S(1)}, f32[1,2048]{1,0:T(1,128)}, u32[]{:S(2)}) copy-start(f32[1,2048]{1,0:T(1,128)} %copy-done.13) | copy-start | bytes 24580
Sparse Core Ops, SparseCore 0:
  9.9 40.1 all-gather.29
  52.5 37.3 all-gather.31
  91.7 37.3 all-gather.33
  130.7 37.3 all-gather.37
  170.3 37.3 all-gather.35
  210.0 37.3 all-gather.39
  250.8 77.4 reduce-scatter.22
  382.1 77.4 reduce-scatter.24
  463.0 77.4 reduce-scatter.18
  543.8 77.4 reduce-scatter.20
  624.7 77.4 reduce-scatter.26
  705.5 77.4 reduce-scatter.28
where the time goes:
time: 800 us; the launch traced here: 793 us
  matrix products  342 us (43%)
  waiting for transfers between devices  313 us (39%)
  other arithmetic  85.2 us (11%)
  local copies, waits for them, and re-layouts  37.6 us (5%)
  between operations  14.9 us (2%)
    unnamed x18, waiting for transfers between devices  237 us
    dot_general x6, matrix products, layer(): up = jnp.dot(a, w['w_up'], preferred_element_type=jnp.float32)  128 us
    dot_general x6, matrix products, layer(): gate = jnp.dot(a, w['w_gate'], preferred_element_type=jnp.float32)  114 us
    dot_general x5, matrix products, matmul(): jnp.dot(a, w, preferred_element_type=jnp.float32).astype(jnp.bfloat16)  99.7 us
    squeeze x6, waiting for transfers between devices, stack(): h = layer(h, {name: w[number] for name, w in weights.items()})  76.3 us
    unnamed x3, other arithmetic  62.6 us
    unnamed x37, local copies, waits for them, and re-layouts  30 us
  transfers between devices with their start and end apart: 12, of which 7 were waited for; matrix products, arithmetic and copies ran while one was open for 57% of the time, Pallas kernels for 0%

commit v1 on v0

v1 whole, which is shorter than its diff:
```python
import jax
import jax.numpy as jnp
from jax import lax
from jax.experimental import pallas as pl
from jax.experimental.pallas import tpu as pltpu
from jax.sharding import PartitionSpec as P

BF, F32 = jnp.bfloat16, jnp.float32
T, D, FF = 2048, 1024, 2816
H = FF // 2
GROWS, DROWS = D // 8, FF // 8
UNITS = ((0, 0), (0, 1), (0, 2), (1, 2), (1, 0), (1, 1))
NT = (((1,), (1,)), ((), ()))
TN = (((0,), (0,)), ((), ()))
VMEM = pltpu.VMEM
ANY = pl.ANY
MIB = 1 << 20


def rows_of(u):
    return DROWS if UNITS[u][1] == 2 else GROWS


def full_shape(u):
    return (FF, D) if UNITS[u][1] == 2 else (D, FF)


def sigmoid(z):
    return 0.5 * jnp.tanh(0.5 * z) + 0.5


def dot(a, b):
    return jnp.dot(a, b, preferred_element_type=F32)


def dotg(a, b, dims):
    return lax.dot_general(a, b, dims, preferred_element_type=F32)


def places():
    me = lax.axis_index("dp")
    ix, iy, ic = me // 4, (me // 2) % 2, me % 2
    flip = lambda a, b, c: (ix + a - 2 * a * ix) * 4 + (iy + b - 2 * b * iy) * 2 + (ic + c - 2 * c * ic)
    return me, flip


def barrier(peers):
    sem = pltpu.get_barrier_semaphore()
    for p in peers:
        pl.semaphore_signal(sem, inc=1, device_id={"dp": p}, device_id_type=pl.DeviceIdType.MESH)
    pl.semaphore_wait(sem, len(peers))


def remote(src, dst, send, recv, to):
    return pltpu.make_async_remote_copy(src_ref=src, dst_ref=dst, send_sem=send, recv_sem=recv, device_id={"dp": to}, device_id_type=pl.DeviceIdType.MESH)


def block(rows, cols, index):
    return pl.BlockSpec((rows, cols), index)


def forward_kernel(x, dy, wg, wu, wd, *refs):
    full, refs = refs[:6], refs[6:]
    a0, a0t, h1, a1, a1t, act0, gu0, act1, dgu1, dact1, mixed, resident, down, send, recv, local, extra, mix = refs
    shards = [wd.at[n] if part == 2 else mixed.at[2 * n + part] for n, part in UNITS]
    me, flip = places()
    nx, ny, peer, nxy = flip(1, 0, 0), flip(0, 1, 0), flip(0, 0, 1), flip(1, 1, 0)

    def part(u, b, half=None):
        r = rows_of(u)
        if half is None:
            return full[u].at[pl.ds(b * r, r), :]
        return full[u].at[pl.ds(b * r + half * (r // 2), r // 2), :]

    def copy(u, k):
        own = shards[u]
        src, dst, to = (
            (own, part(u, me), nx),
            (own, part(u, me), ny),
            (own, part(u, me), peer),
            (part(u, nx, 0), part(u, nx, 0), ny),
            (part(u, ny, 1), part(u, ny, 1), nx),
            (part(u, nx), part(u, nx), peer),
            (part(u, ny), part(u, ny), peer),
            (part(u, nxy, 0), part(u, nxy, 0), peer),
            (part(u, nxy, 1), part(u, nxy, 1), peer),
        )[k]
        return remote(src, dst, send.at[u, k], recv.at[u, k], to)

    def own_copy(u):
        return pltpu.make_async_copy(shards[u], part(u, me), local.at[u])

    def start_own(u):
        for k in (0, 1, 2):
            copy(u, k).start()
        own_copy(u).start()

    def forward_one(u):
        copy(u, 0).wait_recv()
        copy(u, 3).start()
        copy(u, 5).start()
        copy(u, 1).wait_recv()
        copy(u, 4).start()
        copy(u, 6).start()

    def forward_two(u):
        copy(u, 3).wait_recv()
        copy(u, 7).start()
        copy(u, 4).wait_recv()
        copy(u, 8).start()

    def arrived(u):
        own_copy(u).wait()
        for k in (2, 5, 6, 7, 8):
            copy(u, k).wait_recv()

    def load(src, dst, n):
        return pltpu.make_async_copy(src, dst, extra.at[n])

    def norm_into(wide, a_ref, at_ref):
        scale = lax.rsqrt(jnp.mean(wide * wide, -1, keepdims=True) + 1e-6)
        a = wide * scale
        a_ref[...] = a.astype(BF)
        at_ref[...] = a.astype(BF).T

    def mix_start(u):
        n, part = UNITS[u]
        for j in range(11):
            cols = pl.ds(128 * (11 * part + j), 128)
            pltpu.make_async_copy(wg.at[n, :, cols], shards[u].at[:, pl.ds(256 * j, 128)], mix.at[u]).start()
            pltpu.make_async_copy(wu.at[n, :, cols], shards[u].at[:, pl.ds(256 * j + 128, 128)], mix.at[u]).start()

    def mix_wait(u):
        pltpu.make_async_copy(shards[u], shards[u], mix.at[u]).wait()

    for u in (0, 1, 4, 5):
        mix_start(u)
    barrier((nx, ny, peer))
    mix_wait(0)
    start_own(0)
    mix_wait(1)
    start_own(1)
    mix_wait(4)
    mix_wait(5)

    def norm_body(x_ref, a_ref, at_ref):
        norm_into(x_ref[...].astype(F32), a_ref, at_ref)

    pltpu.emit_pipeline(
        norm_body,
        grid=(T // 256,),
        in_specs=[block(256, D, lambda i: (i, 0))],
        out_specs=[block(256, D, lambda i: (i, 0)), block(D, 256, lambda i: (0, i))],
    )(x, a0, a0t)
    load(a0, resident, 0).start()

    forward_one(0)
    start_own(2)
    forward_two(0)
    forward_one(1)
    start_own(3)
    arrived(0)
    load(a0, resident, 0).wait()

    def gu0_body(w_ref, gu_ref, act_ref):
        for m in range(0, T, 512):
            s = dot(resident[m : m + 512, :], w_ref[...])
            gu_ref[m : m + 512, :] = s
            g, up = s[:, :128], s[:, 128:]
            act_ref[m : m + 512, :] = (g * sigmoid(g) * up).astype(BF)

    def gu0_op(half):
        pltpu.emit_pipeline(
            gu0_body,
            grid=(11,),
            in_specs=[block(D, 256, lambda j: (0, j))],
            out_specs=[block(T, 256, lambda j: (0, j + 11 * half)), block(T, 128, lambda j: (0, j + 11 * half))],
        )(full[half], gu0, act0)

    gu0_op(0)
    forward_two(1)
    forward_one(2)
    start_own(4)
    arrived(1)
    gu0_op(1)
    forward_two(2)
    forward_one(3)
    start_own(5)
    arrived(2)
    load(full[2], down, 1).start()
    load(dy, resident, 0).start()
    load(full[2], down, 1).wait()

    def down_body(act_ref, x_ref, h_ref, a_ref, at_ref):
        h = x_ref[...] + dot(act_ref[...], down[...]).astype(BF)
        h_ref[...] = h
        norm_into(h.astype(F32), a_ref, at_ref)

    tile = lambda i: (i, 0)
    pltpu.emit_pipeline(
        down_body,
        grid=(T // 512,),
        in_specs=[block(512, FF, tile), block(512, D, tile)],
        out_specs=[block(512, D, tile), block(512, D, tile), block(D, 512, lambda i: (0, i))],
    )(act0, x, h1, a1, a1t)
    load(dy, resident, 0).wait()
    forward_two(3)
    forward_one(4)
    arrived(3)

    def dact_body(w_ref, out_ref):
        for m in range(0, T, 512):
            out_ref[m : m + 512, :] = dotg(resident[m : m + 512, :], w_ref[...], NT).astype(BF)

    pltpu.emit_pipeline(
        dact_body,
        grid=(11,),
        in_specs=[block(256, D, lambda j: (j, 0))],
        out_specs=[block(T, 256, lambda j: (0, j))],
    )(full[3], dact1)
    load(a1, resident, 0).start()
    forward_two(4)
    forward_one(5)
    arrived(4)
    load(a1, resident, 0).wait()

    def gu1_body(w_ref, dact_ref, act_ref, dgu_ref):
        for m in range(0, T, 512):
            s = dot(resident[m : m + 512, :], w_ref[...])
            g, up = s[:, :128], s[:, 128:]
            d = dact_ref[m : m + 512, :].astype(F32)
            sg = sigmoid(g)
            silu = g * sg
            act_ref[m : m + 512, :] = (silu * up).astype(BF)
            dgu_ref[m : m + 512, :128] = (d * up * (sg + silu * (1.0 - sg))).astype(BF)
            dgu_ref[m : m + 512, 128:] = (d * silu).astype(BF)

    def gu1_op(half):
        col = lambda j: (0, j + 11 * half)
        pltpu.emit_pipeline(
            gu1_body,
            grid=(11,),
            in_specs=[block(D, 256, lambda j: (0, j)), block(T, 128, col)],
            out_specs=[block(T, 128, col), block(T, 256, col)],
        )(full[4 + half], dact1, act1, dgu1)

    gu1_op(0)
    forward_two(5)
    arrived(5)
    gu1_op(1)
    for u in range(6):
        for k in range(9):
            copy(u, k).wait_send()


def forward(x, dy, wg, wu, wd):
    vm, any_ = pl.BlockSpec(memory_space=VMEM), pl.BlockSpec(memory_space=ANY)
    s = jax.ShapeDtypeStruct
    outs = [s(full_shape(u), BF) for u in range(6)]
    outs += [s((T, D), BF), s((D, T), BF), s((T, D), BF), s((T, D), BF), s((D, T), BF)]
    outs += [s((T, FF), BF), s((T, 2 * FF), F32), s((T, FF), BF), s((T, 2 * FF), BF), s((T, FF), BF)]
    return pl.pallas_call(
        forward_kernel,
        out_shape=outs,
        in_specs=[any_, any_, any_, any_, vm],
        out_specs=[any_] * len(outs),
        scratch_shapes=[
            VMEM((4, GROWS, FF), BF),
            VMEM((T, D), BF),
            VMEM((FF, D), BF),
            pltpu.SemaphoreType.DMA((6, 9)),
            pltpu.SemaphoreType.DMA((6, 9)),
            pltpu.SemaphoreType.DMA((6,)),
            pltpu.SemaphoreType.DMA((2,)),
            pltpu.SemaphoreType.DMA((6,)),
        ],
        compiler_params=pltpu.CompilerParams(collective_id=0, has_side_effects=True, vmem_limit_bytes=60 * MIB),
        name="forward_gather",
    )(x, dy, wg, wu, wd)


def backward_kernel(x, h1, dy, a0t, a1t, act0, act1, gu0, dgu1, w00, w01, w02, w10, w11, *refs):
    (by_g, by_u, by_d, dx, dh1, dgu0), term, from_peer, refs = refs[:6], refs[6:12], refs[12:18], refs[18:]
    (weights, resident, resident_t, r1x, r1y, r2x, r2y, d1x, d1y, d2x, d2y, gsend, dsend, gload, dload, send, recv, lsem, extra, osem) = refs
    me, flip = places()
    nx, ny, peer, nxy = flip(1, 0, 0), flip(0, 1, 0), flip(0, 0, 1), flip(1, 1, 0)
    where = (me, nx, ny, nxy)

    def kind(u):
        return UNITS[u][1] == 2

    def slot(u):
        return {0: 0, 1: 1, 2: 0, 3: 1, 4: 2, 5: 3}[u]

    def landing(u):
        s = slot(u)
        return tuple(t.at[s] for t in ((d1x, d1y, d2x, d2y) if kind(u) else (r1x, r1y, r2x, r2y)))

    def sending(u):
        return dsend if kind(u) else gsend

    def loading(u):
        return dload if kind(u) else gload

    def peer_block(b):
        return b + 1 - 2 * (b % 2)

    def copy(u, k):
        r = rows_of(u)
        if k < 4:
            b = where[k]
            return remote(term[u].at[pl.ds(peer_block(b) * r, r), :], from_peer[u].at[pl.ds((b // 2) * r, r), :], send.at[u, k], recv.at[u, k], peer)
        s, (l1x, l1y, l2x, l2y) = sending(u), landing(u)
        half = r // 2
        src, dst, to = {
            4: (s.at[0, pl.ds(0, half), :], l1x, nx),
            5: (s.at[0, pl.ds(half, half), :], l1y, ny),
            6: (s.at[1], l2x, nx),
            7: (s.at[2], l2y, ny),
        }[k]
        return remote(src, dst, send.at[u, k], recv.at[u, k], to)

    def pair(u, q, n):
        r = rows_of(u)
        b = where[q]
        v = loading(u)
        return (
            pltpu.make_async_copy(term[u].at[pl.ds(b * r, r), :], v.at[n], lsem.at[2 * n]),
            pltpu.make_async_copy(from_peer[u].at[pl.ds((b // 2) * r, r), :], v.at[n + 2], lsem.at[2 * n + 1]),
        )

    def send_term(u):
        for k in range(4):
            copy(u, k).start()

    def fetch(u, *qs):
        copies = [c for n, q in enumerate(qs) for c in pair(u, q, n)]
        for q in qs:
            copy(u, q).wait_recv()
        for c in copies:
            c.start()
        for c in copies:
            c.wait()

    in_flight = {(k, n): None for k in (False, True) for n in (4, 5, 6, 7)}

    def sent_before(u, *ks):
        for k in ks:
            if in_flight[kind(u), k] is not None:
                copy(in_flight[kind(u), k], k).wait_send()

    def ship(u, *ks):
        for k in ks:
            copy(u, k).start()
            in_flight[kind(u), k] = u

    def chunks(u, body):
        step = 16
        lax.fori_loop(0, rows_of(u) // step, lambda i, _: (body(pl.ds(pl.multiple_of(i * step, step), step)), 0)[1], 0)

    def chunks2(u, body):
        step = 16
        lax.fori_loop(0, rows_of(u) // 2 // step, lambda i, _: (body(pl.multiple_of(i * step, step)), 0)[1], 0)

    def both(v, q, rows):
        return v[q, rows, :].astype(F32) + v[q + 2, rows, :].astype(F32)

    def pass1(u):
        fetch(u, 3)
        v, s = loading(u), sending(u)
        sent_before(u, 4, 5)

        def body(rows):
            s[0, rows, :] = both(v, 0, rows).astype(BF)

        chunks(u, body)
        ship(u, 4, 5)

    def pass2(u):
        fetch(u, 1, 2)
        v, s = loading(u), sending(u)
        l1x, l1y, _, _ = landing(u)
        sent_before(u, 6, 7)
        half = rows_of(u) // 2
        copy(u, 4).wait_recv()
        copy(u, 5).wait_recv()

        def body(at):
            low, high = pl.ds(at, 16), pl.ds(at + half, 16)
            s[1, low, :] = both(v, 0, low).astype(BF)
            s[1, high, :] = (both(v, 0, high) + l1y[low, :].astype(F32)).astype(BF)
            s[2, low, :] = (both(v, 1, low) + l1x[low, :].astype(F32)).astype(BF)
            s[2, high, :] = both(v, 1, high).astype(BF)

        chunks2(u, body)
        ship(u, 6, 7)

    def pass3(u):
        fetch(u, 0)
        v = loading(u)
        _, _, l2x, l2y = landing(u)
        copy(u, 6).wait_recv()
        copy(u, 7).wait_recv()

        n, half = UNITS[u]

        def body(rows):
            total = both(v, 0, rows) + l2x[rows, :].astype(F32) + l2y[rows, :].astype(F32)
            if kind(u):
                v[1, rows, :] = total.astype(BF)
                return
            for j in range(11):
                v[1, rows, 128 * j : 128 * j + 128] = total[:, 256 * j : 256 * j + 128].astype(BF)
                v[1, rows, H + 128 * j : H + 128 * j + 128] = total[:, 256 * j + 128 : 256 * j + 256].astype(BF)

        chunks(u, body)
        if kind(u):
            copies = [pltpu.make_async_copy(v.at[1], by_d.at[n], osem.at[0])]
        else:
            cols = pl.ds(half * H, H)
            copies = [
                pltpu.make_async_copy(v.at[1, :, pl.ds(0, H)], by_g.at[n, :, cols], osem.at[0]),
                pltpu.make_async_copy(v.at[1, :, pl.ds(H, H)], by_u.at[n, :, cols], osem.at[1]),
            ]
        for c in copies:
            c.start()
        for c in copies:
            c.wait()

    def load(src, dst, n):
        return pltpu.make_async_copy(src, dst, extra.at[n])

    def grad_gu(u, dgu):
        half = UNITS[u][1]

        def body(d_ref, out_ref):
            for m in range(0, D, 512):
                out_ref[m : m + 512, :] = dot(resident_t[m : m + 512, :], d_ref[...]).astype(BF)

        pltpu.emit_pipeline(
            body,
            grid=(11,),
            in_specs=[block(T, 256, lambda j: (0, j + 11 * half))],
            out_specs=[block(D, 256, lambda j: (0, j))],
        )(dgu, term[u])

    def grad_down(u, act):
        def body(act_ref, out_ref):
            out_ref[...] = dotg(act_ref[...], resident[...], TN).astype(BF)

        pltpu.emit_pipeline(
            body,
            grid=(11,),
            in_specs=[block(T, 256, lambda j: (0, j))],
            out_specs=[block(256, D, lambda j: (j, 0))],
        )(act, term[u])

    def grad_in(dgu, h, dh, out, first, count):
        def body(d_ref, h_ref, dh_ref, out_ref):
            da = dotg(d_ref[:, :FF], weights[0], NT) + dotg(d_ref[:, FF:], weights[1], NT)
            d = da.astype(BF).astype(F32)
            wide = h_ref[...].astype(F32)
            scale = lax.rsqrt(jnp.mean(wide * wide, -1, keepdims=True) + 1e-6)
            by_h = d * scale - wide * (scale * scale * scale * jnp.mean(d * wide, -1, keepdims=True))
            out_ref[...] = dh_ref[...] + by_h.astype(BF)

        t = lambda i: (i + first, 0)
        pltpu.emit_pipeline(
            body,
            grid=(count,),
            in_specs=[block(256, 2 * FF, t), block(256, D, t), block(256, D, t)],
            out_specs=[block(256, D, t)],
        )(dgu, h, dh, out)

    def act_back(w, gu, dgu):
        def body(w_ref, gu_ref, dgu_ref):
            for m in range(0, T, 512):
                rows = slice(m, m + 512)
                dd = dotg(resident[rows, :], w_ref[...], NT).astype(BF).astype(F32)
                for n in range(2):
                    g = gu_ref[rows, 256 * n : 256 * n + 128]
                    up = gu_ref[rows, 256 * n + 128 : 256 * n + 256]
                    d = dd[:, 128 * n : 128 * n + 128]
                    sg = sigmoid(g)
                    silu = g * sg
                    dgu_ref[rows, 256 * n : 256 * n + 128] = (d * up * (sg + silu * (1.0 - sg))).astype(BF)
                    dgu_ref[rows, 256 * n + 128 : 256 * n + 256] = (d * silu).astype(BF)

        pltpu.emit_pipeline(
            body,
            grid=(11,),
            in_specs=[block(256, D, lambda j: (j, 0)), block(T, 512, lambda j: (0, j))],
            out_specs=[block(T, 512, lambda j: (0, j))],
        )(w, gu, dgu)

    barrier((nx, ny, peer))
    loads = [load(a1t, resident_t, 0), load(dy, resident, 1), load(w10, weights.at[0], 2), load(w11, weights.at[1], 3)]
    for c in loads:
        c.start()
    loads[0].wait()
    grad_gu(4, dgu1)
    send_term(4)
    grad_gu(5, dgu1)
    send_term(5)
    again = load(a0t, resident_t, 0)
    again.start()
    pass1(4)
    loads[1].wait()
    grad_down(3, act1)
    send_term(3)
    pass2(4)
    pass1(5)
    loads[2].wait()
    loads[3].wait()
    grad_in(dgu1, h1, dy, dh1, 0, 4)
    pass2(5)
    pass1(3)
    grad_in(dgu1, h1, dy, dh1, 4, 4)
    loads = [load(dh1, resident, 1), load(w00, weights.at[0], 2), load(w01, weights.at[1], 3)]
    for c in loads:
        c.start()
    pass3(4)
    pass2(3)
    loads[0].wait()
    act_back(w02, gu0, dgu0)
    pass3(5)
    grad_down(2, act0)
    send_term(2)
    pass3(3)
    again.wait()
    grad_gu(0, dgu0)
    send_term(0)
    pass1(2)
    grad_gu(1, dgu0)
    send_term(1)
    pass2(2)
    pass1(0)
    loads[1].wait()
    loads[2].wait()
    grad_in(dgu0, x, dh1, dx, 0, 4)
    pass2(0)
    pass1(1)
    grad_in(dgu0, x, dh1, dx, 4, 4)
    pass2(1)
    pass3(2)
    pass3(0)
    pass3(1)
    for (_, k), u in in_flight.items():
        copy(u, k).wait_send()
    for u in range(6):
        for k in range(4):
            copy(u, k).wait_send()


def backward(x, dy, saved):
    full, (_, a0t, h1, _, a1t, act0, gu0, act1, dgu1, _) = saved[:6], saved[6:]
    any_ = pl.BlockSpec(memory_space=ANY)
    s = jax.ShapeDtypeStruct
    outs = [s((2, GROWS, FF), BF)] * 2 + [s((2, DROWS, D), BF)]
    outs += [s((T, D), BF), s((T, D), BF), s((T, 2 * FF), BF)]
    outs += [s(full_shape(u), BF) for u in range(6)]
    outs += [s((4 * rows_of(u), full_shape(u)[1]), BF) for u in range(6)]
    dma = pltpu.SemaphoreType.DMA
    return pl.pallas_call(
        backward_kernel,
        out_shape=outs,
        in_specs=[any_] * 14,
        out_specs=[any_] * len(outs),
        scratch_shapes=[
            VMEM((2, D, FF), BF),
            VMEM((T, D), BF),
            VMEM((D, T), BF),
            *[VMEM((4, GROWS // 2, FF), BF)] * 2,
            *[VMEM((4, GROWS, FF), BF)] * 2,
            *[VMEM((2, DROWS // 2, D), BF)] * 2,
            *[VMEM((2, DROWS, D), BF)] * 2,
            VMEM((3, GROWS, FF), BF),
            VMEM((3, DROWS, D), BF),
            VMEM((4, GROWS, FF), BF),
            VMEM((4, DROWS, D), BF),
            dma((6, 8)),
            dma((6, 8)),
            dma((4,)),
            dma((4,)),
            dma((2,)),
        ],
        compiler_params=pltpu.CompilerParams(collective_id=1, has_side_effects=True, vmem_limit_bytes=63 * MIB),
        name="backward_scatter",
    )(x, h1, dy, a0t, a1t, act0, act1, gu0, dgu1, full[0], full[1], full[2], full[4], full[5])


def solution(mesh):
    def body(x, dy, wg, wu, wd):
        x, dy = x[0], dy[0]
        saved = forward(x, dy, wg, wu, wd)
        by_g, by_u, by_d, dx = backward(x, dy, saved)[:4]
        return dx[None], by_g, by_u, by_d

    seq, rows = P(("rep", "dp"), None, None), P(None, "dp", None)
    out = P("rep", "dp", None)
    return jax.shard_map(body, mesh=mesh, in_specs=(seq, seq, rows, rows, rows), out_specs=(seq, out, out, out), check_vma=False)
```

time: 800 us -> 475 us (0.59)
  Pallas kernels: 0 us -> 462 us
  matrix products: 342 us -> 0 us
  waiting for transfers between devices: 313 us -> 0 us
  other arithmetic: 85.2 us -> 0 us
  local copies, waits for them, and re-layouts: 37.6 us -> 8.11 us
  between operations: 14.9 us -> 0.67 us
    pallas_call x0 -> x2, Pallas kernels: none -> 462 us  [the longest x1 276 us: backward(): pl.pallas_call(backward_kernel, out_shape=outs, in_specs=[any_] * 14, out...]
    dot_general x17 -> x0, matrix products: 342 us -> none  [the longest x6 128 us: layer(): up = jnp.dot(a, w['w_up'], preferred_element_type=jnp.float32)]
    unnamed x18 -> x0, waiting for transfers between devices: 237 us -> none
    squeeze x6 -> x0, waiting for transfers between devices: 76.3 us -> none  [stack(): h = layer(h, {name: w[number] for name, w in weights.items()})]
    unnamed x3 -> x0, other arithmetic: 62.6 us -> none
    unnamed x37 -> x10, local copies, waits for them, and re-layouts: 30 us -> 8.11 us
    add_any x2 -> x0, other arithmetic: 9.4 us -> none  [normed(): wide = h.astype(jnp.float32)]
    broadcast_in_dim x6 -> x0, other arithmetic: 8.66 us -> none  [stack(): h = layer(h, {name: w[number] for name, w in weights.items()})]
  transfers between devices with their start and end apart: 12 -> 0, of which waited for: 7 -> 0; matrix products, arithmetic and copies ran while one was open for 57% -> 0% of each run, Pallas kernels for 0% -> 0%
where the time goes in v1:
time: 475 us; the launch traced here: 471 us
  Pallas kernels  462 us (97%)
  local copies, waits for them, and re-layouts  8.11 us (2%)
    pallas_call x1, Pallas kernels, backward(): pl.pallas_call(backward_kernel, out_shape=outs, in_specs=[any_] * 14, out...  276 us
    pallas_call x1, Pallas kernels, forward(): pl.pallas_call(forward_kernel, out_shape=outs, in_specs=[any_, any_, any_...  185 us

profile of v1, /device:TPU:0, one launch (start us, length us, event | category | flops | bytes accessed | tf_op | source)
XLA Modules:
  0.0 470.5 jit_solution(12034485223302835613)
XLA Ops:
  0.6 185.3 %forward_gather.1 = (bf16[1024,2816]{1,0:T(8,128)(2,1)}, bf16[1024,2816]{1,0:T(8,128)(2,1)}, bf16[2816,1024]{1,0:T(8,128)(2,1)}, bf16[2816,1024]{1,0:T(8,128)(2,...) custom-call(bf16[2048,1024]{1,0:T(8,128)(2,1)} %bitcast.3, ...), custom_call_target="tpu_custom_call" | custom-call | tf_op jit(solution)/shard_map/forward_gather/pallas_call | solution.py:262
  185.9 276.4 %backward_scatter.1 = (bf16[2,128,2816]{2,1,0:T(8,128)(2,1)}, bf16[2,128,2816]{2,1,0:T(8,128)(2,1)}, bf16[2,352,1024]{2,1,0:T(8,128)(2,1)}, bf16[2048,1024]{1,0:...) custom-call(bf16[2048,1024]{1,0:T(8,128)(2,1)} %bitcast.4, ...), custom_call_target="tpu_custom_call" | custom-call | tf_op jit(solution)/shard_map/backward_scatter/pallas_call | solution.py:564
  462.4 0.0 copy-start.2
  462.4 0.0 copy-start.1
  462.4 4.8 %copy.13 = bf16[1,2048,1024]{2,1,0:T(8,128)(2,1)} copy(bf16[1,2048,1024]{2,1,0:T(8,128)(2,1)} %bitcast.7) | data formatting | bytes 8388608
  467.2 0.0 copy-done.2
  467.2 0.0 copy-start
  467.2 1.1 copy.14
  468.3 0.0 copy-done.1
  468.3 1.1 copy.15
  469.4 0.0 copy-done
  469.4 1.1 copy.16
Async XLA Ops:
  462.4 4.8 %copy-start.2 = (bf16[2,128,2816]{2,1,0:T(8,128)(2,1)S(1)}, bf16[2,128,2816]{2,1,0:T(8,128)(2,1)}, u32[]{:S(2)}) copy-start(bf16[2,128,2816]{2,1,0:T(8,128)(2,1)} %get-tuple-element.41) | copy-start | bytes 4325380
  462.4 5.9 %copy-start.1 = (bf16[2,128,2816]{2,1,0:T(8,128)(2,1)S(1)}, bf16[2,128,2816]{2,1,0:T(8,128)(2,1)}, u32[]{:S(2)}) copy-start(bf16[2,128,2816]{2,1,0:T(8,128)(2,1)} %get-tuple-element.42) | copy-start | bytes 4325380
  467.2 2.2 copy-start

commit v2 on v0

v2 whole, which is shorter than its diff:
```python
import jax
import jax.numpy as jnp
from jax import lax
from jax.experimental import pallas as pl
from jax.experimental.pallas import tpu as pltpu
from jax.sharding import PartitionSpec as P

BF, F32 = jnp.bfloat16, jnp.float32
T, D, FF = 2048, 1024, 2816
H = FF // 2
GROWS, DROWS = D // 8, FF // 8
UNITS = ((0, 0), (0, 1), (0, 2), (1, 2), (1, 0), (1, 1))
NT = (((1,), (1,)), ((), ()))
TN = (((0,), (0,)), ((), ()))
VMEM = pltpu.VMEM
ANY = pl.ANY
L, W, M = 128, 256, 512
STEPS = FF // W


def rows_of(u):
    return DROWS if UNITS[u][1] == 2 else GROWS


def full_shape(u):
    return (FF, D) if UNITS[u][1] == 2 else (D, FF)


def sigmoid(z):
    return 0.5 * jnp.tanh(0.5 * z) + 0.5


def dot(a, b):
    return jnp.dot(a, b, preferred_element_type=F32)


def dotg(a, b, dims):
    return lax.dot_general(a, b, dims, preferred_element_type=F32)


def places():
    me = lax.axis_index("dp")
    ix, iy, ic = me // 4, (me // 2) % 2, me % 2
    flip = lambda a, b, c: (ix + a - 2 * a * ix) * 4 + (iy + b - 2 * b * iy) * 2 + (ic + c - 2 * c * ic)
    return me, flip


def barrier(peers):
    sem = pltpu.get_barrier_semaphore()
    for p in peers:
        pl.semaphore_signal(sem, inc=1, device_id={"dp": p}, device_id_type=pl.DeviceIdType.MESH)
    pl.semaphore_wait(sem, len(peers))


def remote(src, dst, send, recv, to):
    return pltpu.make_async_remote_copy(src_ref=src, dst_ref=dst, send_sem=send, recv_sem=recv, device_id={"dp": to}, device_id_type=pl.DeviceIdType.MESH)


def block(rows, cols, index):
    return pl.BlockSpec((rows, cols), index)


def row(i):
    return i, 0


def col(j):
    return 0, j


def pipeline(body, grid, ins, outs, hooks, *arrays):
    def run(*refs):
        step = pl.program_id(0)
        if len(grid) == 2:
            step = step * grid[1] + pl.program_id(1)
        for at, work in (hooks or {}).items():
            pl.when(step == at)(work)
        body(*refs)

    pltpu.emit_pipeline(run, grid=grid, in_specs=ins, out_specs=outs)(*arrays)


def inverse_rms(wide):
    return lax.rsqrt(jnp.mean(wide * wide, -1, keepdims=True) + 1e-6)


def kernel(x, dy, wg, wu, wd, *refs):
    (by_g, by_u, by_d, dx), refs = refs[:4], refs[4:]
    full, term, from_peer, refs = refs[:6], refs[6:12], refs[12:18], refs[18:]
    a0, a0t, h1, a1, a1t, act0, gu0, act1, dgu1, dact1, dh1, dgu0, refs = *refs[:12], refs[12:]
    weights, down, resident, resident_t, *landings, gsend, dsend, gload, dload, gsem, gsem2, send, recv, local, mix, extra, lsem, osem = refs
    me, flip = places()
    nx, ny, peer, nxy = flip(1, 0, 0), flip(0, 1, 0), flip(0, 0, 1), flip(1, 1, 0)
    shards = [wd.at[n] if part == 2 else gload.at[2 * n + part] for n, part in UNITS]

    def load(src, dst, n):
        return pltpu.make_async_copy(src, dst, extra.at[n])


    def part(u, b, half=None):
        r = rows_of(u)
        if half is None:
            return full[u].at[pl.ds(b * r, r), :]
        return full[u].at[pl.ds(b * r + half * (r // 2), r // 2), :]

    def hop(u, k):
        src, dst, to = (
            (shards[u], part(u, me), nx),
            (shards[u], part(u, me), ny),
            (shards[u], part(u, me), peer),
            (part(u, nx, 0), part(u, nx, 0), ny),
            (part(u, ny, 1), part(u, ny, 1), nx),
            (part(u, nx), part(u, nx), peer),
            (part(u, ny), part(u, ny), peer),
            (part(u, nxy, 0), part(u, nxy, 0), peer),
            (part(u, nxy, 1), part(u, nxy, 1), peer),
        )[k]
        return remote(src, dst, gsem.at[u, k], gsem2.at[u, k], to)

    def own_copy(u):
        return pltpu.make_async_copy(shards[u], part(u, me), local.at[u])

    def start_own(u):
        for k in range(3):
            hop(u, k).start()
        own_copy(u).start()

    def pass_on(u):
        for k in (0, 1):
            hop(u, k).wait_recv()
            hop(u, k + 3).start()
            hop(u, k + 5).start()

    def pass_on_last(u):
        for k in (3, 4):
            hop(u, k).wait_recv()
            hop(u, k + 4).start()

    def arrived(u):
        own_copy(u).wait()
        for k in (2, 5, 6, 7, 8):
            hop(u, k).wait_recv()

    def mix_start(u):
        n, half = UNITS[u]
        for j in range(STEPS):
            cols = pl.ds(half * H + L * j, L)
            for i, w in enumerate((wg, wu)):
                pltpu.make_async_copy(w.at[n, :, cols], shards[u].at[:, pl.ds(W * j + L * i, L)], mix.at[u]).start()

    def mix_wait(u):
        pltpu.make_async_copy(shards[u], shards[u], mix.at[u]).wait()

    where = (me, nx, ny, nxy)

    def kind(u):
        return UNITS[u][1] == 2

    slot = (0, 1, 0, 1, 2, 3)
    before = {5: 4, 0: 5, 1: 0, 2: 3}

    def landing(u):
        return tuple(t.at[slot[u]] for t in landings[4 * kind(u) : 4 * kind(u) + 4])

    def sending(u):
        return dsend if kind(u) else gsend

    def loading(u):
        return dload if kind(u) else gload

    def copy(u, k):
        r = rows_of(u)
        if k < 4:
            b = where[k]
            other = b + 1 - 2 * (b % 2)
            return remote(term[u].at[pl.ds(other * r, r), :], from_peer[u].at[pl.ds((b // 2) * r, r), :], send.at[u, k], recv.at[u, k], peer)
        s, (l1x, l1y, l2x, l2y) = sending(u), landing(u)
        half = r // 2
        src, dst, to = (
            (s.at[0, pl.ds(0, half), :], l1x, nx),
            (s.at[0, pl.ds(half, half), :], l1y, ny),
            (s.at[1], l2x, nx),
            (s.at[2], l2y, ny),
        )[k - 4]
        return remote(src, dst, send.at[u, k], recv.at[u, k], to)

    def send_term(u):
        for k in (3, 1, 2, 0):
            copy(u, k).start()

    def pairs(u, qs):
        r, v = rows_of(u), loading(u)
        for n, q in enumerate(qs):
            b = where[q]
            yield pltpu.make_async_copy(term[u].at[pl.ds(b * r, r), :], v.at[n], lsem.at[2 * n])
            yield pltpu.make_async_copy(from_peer[u].at[pl.ds((b // 2) * r, r), :], v.at[n + 2], lsem.at[2 * n + 1])

    def fetch(u, *qs):
        for q in qs:
            copy(u, q).wait_recv()
        for c in pairs(u, qs):
            c.start()

    def fetched(u, *qs):
        for c in pairs(u, qs):
            c.wait()

    def chunks(count, body):
        def step(i, _):
            body(pl.multiple_of(i * 16, 16))
            return 0

        lax.fori_loop(0, count // 16, step, 0)

    def both(v, n, rows):
        return v[n, rows, :].astype(F32) + v[n + 2, rows, :].astype(F32)

    def sent_before(u, *ks):
        if u in before:
            for k in ks:
                copy(before[u], k).wait_send()

    def fetch1(u):
        return lambda: fetch(u, 3)

    def fetch2(u):
        return lambda: fetch(u, 1, 2)

    def fetch3(u):
        return lambda: fetch(u, 0)

    def pass1(u):
        def work():
            fetched(u, 3)
            v, s = loading(u), sending(u)
            sent_before(u, 4, 5)

            def body(at):
                rows = pl.ds(at, 16)
                s[0, rows, :] = both(v, 0, rows).astype(BF)

            chunks(rows_of(u), body)
            copy(u, 4).start()
            copy(u, 5).start()

        return work

    def pass2(u):
        def work():
            fetched(u, 1, 2)
            v, s = loading(u), sending(u)
            l1x, l1y, _, _ = landing(u)
            sent_before(u, 6, 7)
            half = rows_of(u) // 2
            copy(u, 4).wait_recv()
            copy(u, 5).wait_recv()

            def body(at):
                low, high = pl.ds(at, 16), pl.ds(at + half, 16)
                s[1, low, :] = both(v, 0, low).astype(BF)
                s[1, high, :] = (both(v, 0, high) + l1y[low, :].astype(F32)).astype(BF)
                s[2, low, :] = (both(v, 1, low) + l1x[low, :].astype(F32)).astype(BF)
                s[2, high, :] = both(v, 1, high).astype(BF)

            chunks(half, body)
            copy(u, 6).start()
            copy(u, 7).start()

        return work

    def pass3(u):
        def work():
            fetched(u, 0)
            v = loading(u)
            _, _, l2x, l2y = landing(u)
            copy(u, 6).wait_recv()
            copy(u, 7).wait_recv()
            n, half = UNITS[u]

            def body(at):
                rows = pl.ds(at, 16)
                total = (both(v, 0, rows) + l2x[rows, :].astype(F32) + l2y[rows, :].astype(F32)).astype(BF)
                if kind(u):
                    v[1, rows, :] = total
                    return
                for j in range(STEPS):
                    for i in range(2):
                        v[1, rows, H * i + L * j : H * i + L * j + L] = total[:, W * j + L * i : W * j + L * i + L]

            chunks(rows_of(u), body)
            if kind(u):
                copies = [pltpu.make_async_copy(v.at[1], by_d.at[n], osem.at[0])]
            else:
                cols = pl.ds(half * H, H)
                copies = [pltpu.make_async_copy(v.at[1, :, pl.ds(H * i, H)], t.at[n, :, cols], osem.at[i]) for i, t in enumerate((by_g, by_u))]
            for c in copies:
                c.start()
            for c in copies:
                c.wait()

        return work

    def together(*works):
        def work():
            for w in works:
                w()

        return work


    def norm_into(wide, a_ref, at_ref):
        a = (wide * inverse_rms(wide)).astype(BF)
        a_ref[...] = a
        at_ref[...] = a.T

    def norm_body(x_ref, a_ref, at_ref):
        norm_into(x_ref[...].astype(F32), a_ref, at_ref)

    def gate_up0(half):
        def body(w_ref, gu_ref, act_ref):
            for m in range(0, T, M):
                s = dot(resident[m : m + M, :], w_ref[...])
                gu_ref[m : m + M, :] = s
                g, up = s[:, :L], s[:, L:]
                act_ref[m : m + M, :] = (g * sigmoid(g) * up).astype(BF)

        cols = lambda j: (0, j + STEPS * half)
        pipeline(body, (STEPS,), [block(D, W, col)], [block(T, W, cols), block(T, L, cols)], None, full[half], gu0, act0)

    def down_body(act_ref, x_ref, h_ref, a_ref, at_ref):
        h = x_ref[...] + dot(act_ref[...], down[...]).astype(BF)
        h_ref[...] = h
        norm_into(h.astype(F32), a_ref, at_ref)

    def dact_body(w_ref, out_ref):
        for m in range(0, T, M):
            out_ref[m : m + M, :] = dotg(resident[m : m + M, :], w_ref[...], NT).astype(BF)

    def back(g, up, d):
        sg = sigmoid(g)
        silu = g * sg
        return silu, (d * up * (sg + silu * (1.0 - sg))).astype(BF), (d * silu).astype(BF)

    def gate_up1(half, hooks):
        def body(w_ref, dact_ref, act_ref, dgu_ref):
            for m in range(0, T, M):
                rows = slice(m, m + M)
                s = dot(resident[rows, :], w_ref[...])
                up = s[:, L:]
                silu, dg, du = back(s[:, :L], up, dact_ref[rows, :].astype(F32))
                act_ref[rows, :] = (silu * up).astype(BF)
                dgu_ref[rows, :L] = dg
                dgu_ref[rows, L:] = du

        cols = lambda j: (0, j + STEPS * half)
        ins, outs = [block(D, W, col), block(T, L, cols)], [block(T, L, cols), block(T, W, cols)]
        pipeline(body, (STEPS,), ins, outs, hooks, full[4 + half], dact1, act1, dgu1)

    def grad_gu(u, dgu, hooks):
        half = UNITS[u][1]

        def body(d_ref, out_ref):
            for m in range(0, D, M):
                out_ref[m : m + M, :] = dot(resident_t[m : m + M, :], d_ref[...]).astype(BF)

        pipeline(body, (STEPS,), [block(T, W, lambda j: (0, j + STEPS * half))], [block(D, W, col)], hooks, dgu, term[u])
        send_term(u)

    def grad_down(u, act, hooks):
        def body(act_ref, out_ref):
            out_ref[...] = dotg(act_ref[...], resident[...], TN).astype(BF)

        pipeline(body, (STEPS,), [block(T, W, col)], [block(W, D, row)], hooks, act, term[u])
        send_term(u)

    def grad_in(dgu, h, dh, out, keep, hooks):
        def body(d_ref, h_ref, dh_ref, out_ref):
            da = dotg(d_ref[:, :FF], weights[0], NT) + dotg(d_ref[:, FF:], weights[1], NT)
            d = da.astype(BF).astype(F32)
            wide = h_ref[...].astype(F32)
            scale = inverse_rms(wide)
            by_h = d * scale - wide * (scale * scale * scale * jnp.mean(d * wide, -1, keepdims=True))
            total = dh_ref[...] + by_h.astype(BF)
            out_ref[...] = total
            if keep:
                resident[pl.ds(pl.multiple_of(pl.program_id(0) * W, W), W), :] = total

        pipeline(body, (T // W,), [block(W, 2 * FF, row)] + [block(W, D, row)] * 2, [block(W, D, row)], hooks, dgu, h, dh, out)

    def act_back(hooks):
        def body(w_ref, gu_ref, dgu_ref):
            first = pl.program_id(0) * (T // 2)
            for m in range(0, T // 2, M):
                rows = slice(m, m + M)
                dd = dotg(resident[pl.ds(pl.multiple_of(first + m, M), M), :], w_ref[...], NT).astype(BF).astype(F32)
                for n in range(2):
                    at = W * n
                    _, dg, du = back(gu_ref[rows, at : at + L], gu_ref[rows, at + L : at + W], dd[:, L * n : L * n + L])
                    dgu_ref[rows, at : at + L] = dg
                    dgu_ref[rows, at + L : at + W] = du

        wide = block(T // 2, M, lambda i, j: (i, j))
        pipeline(body, (2, STEPS), [block(W, D, lambda i, j: (j, 0)), wide], [wide], hooks, full[2], gu0, dgu0)

    for u in (0, 1, 4, 5):
        mix_start(u)
    barrier((nx, ny, peer))
    for u in range(2):
        mix_wait(u)
        start_own(u)
    mix_wait(4)
    mix_wait(5)
    pipeline(norm_body, (T // W,), [block(W, D, row)], [block(W, D, row), block(D, W, col)], None, x, a0, a0t)
    in_a = load(a0, resident, 0)
    in_a.start()
    pass_on(0)
    start_own(2)
    pass_on_last(0)
    pass_on(1)
    start_own(3)
    arrived(0)
    in_a.wait()
    gate_up0(0)
    pass_on_last(1)
    pass_on(2)
    start_own(4)
    arrived(1)
    gate_up0(1)
    in_dy = load(dy, resident, 0)
    in_dy.start()
    pass_on_last(2)
    pass_on(3)
    start_own(5)
    arrived(2)
    in_down = load(full[2], down, 1)
    in_down.start()
    in_down.wait()
    outs = [block(M, D, row), block(M, D, row), block(D, M, col)]
    pipeline(down_body, (T // M,), [block(M, FF, row), block(M, D, row)], outs, None, act0, x, h1, a1, a1t)
    in_at = load(a1t, resident_t, 1)
    in_at.start()
    in_dy.wait()
    pass_on_last(3)
    pass_on(4)
    arrived(3)
    pipeline(dact_body, (STEPS,), [block(W, D, row)], [block(T, W, col)], None, full[3], dact1)
    in_a = load(a1, resident, 0)
    in_a.start()
    pass_on_last(4)
    in_at.wait()
    in_a.wait()
    arrived(4)
    gate_up1(0, {5: lambda: pass_on(5)})
    grad_gu(4, dgu1, None)
    pass_on_last(5)
    arrived(5)
    for u in range(6):
        for k in range(9):
            hop(u, k).wait_send()
    in_w = [load(full[4 + i], weights.at[i], 2 + i) for i in range(2)]
    for c in in_w:
        c.start()
    gate_up1(1, {4: fetch1(4), 6: pass1(4)})
    in_dy = load(dy, resident, 0)
    in_dy.start()
    grad_gu(5, dgu1, {1: fetch2(4), 4: pass2(4)})
    in_at = load(a0t, resident_t, 1)
    in_at.start()
    in_dy.wait()
    grad_down(3, act1, {4: fetch1(5), 6: pass1(5), 7: fetch3(4), 9: pass3(4)})
    for c in in_w:
        c.wait()
    grad_in(dgu1, h1, dy, dh1, True, {0: fetch2(5), 1: together(pass2(5), fetch1(3)), 3: pass1(3), 6: fetch3(5), 7: pass3(5)})
    in_w = [load(full[i], weights.at[i], 2 + i) for i in range(2)]
    for c in in_w:
        c.start()
    grad_down(2, act0, {0: fetch2(3), 2: pass2(3)})
    act_back({4: fetch3(3), 7: together(pass3(3), fetch1(2)), 10: pass1(2)})
    in_at.wait()
    grad_gu(0, dgu0, {0: fetch2(2), 2: pass2(2)})
    grad_gu(1, dgu0, {4: fetch1(0), 6: pass1(0), 7: fetch3(2), 10: pass3(2)})
    for c in in_w:
        c.wait()
    grad_in(dgu0, x, dh1, dx, False, {0: fetch2(0), 1: together(pass2(0), fetch1(1)), 2: pass1(1), 6: fetch3(0), 7: together(pass3(0), fetch2(1))})
    pass2(1)()
    fetch3(1)()
    pass3(1)()
    for u in (1, 2):
        for k in range(4, 8):
            copy(u, k).wait_send()
    for u in range(6):
        for k in range(4):
            copy(u, k).wait_send()


def solution(mesh):
    any_ = pl.BlockSpec(memory_space=ANY)
    dma = pltpu.SemaphoreType.DMA

    def s(*shape, dtype=BF):
        return jax.ShapeDtypeStruct(shape, dtype)

    outs = [s(2, GROWS, FF), s(2, GROWS, FF), s(2, DROWS, D), s(T, D)]
    outs += [s(*full_shape(u)) for u in range(6)] * 2
    outs += [s(4 * rows_of(u), full_shape(u)[1]) for u in range(6)]
    outs += [s(T, D), s(D, T), s(T, D), s(T, D), s(D, T), s(T, FF), s(T, 2 * FF, dtype=F32), s(T, FF), s(T, 2 * FF), s(T, FF), s(T, D), s(T, 2 * FF)]
    scratch = [VMEM((2, D, FF), BF), VMEM((FF, D), BF), VMEM((T, D), BF), VMEM((D, T), BF)]
    scratch += [VMEM((4, r, FF), BF) for r in (GROWS // 2, GROWS // 2, GROWS, GROWS)]
    scratch += [VMEM((2, r, D), BF) for r in (DROWS // 2, DROWS // 2, DROWS, DROWS)]
    scratch += [VMEM((3, GROWS, FF), BF), VMEM((3, DROWS, D), BF), VMEM((4, GROWS, FF), BF), VMEM((4, DROWS, D), BF)]
    scratch += [dma((6, 9)), dma((6, 9)), dma((6, 8)), dma((6, 8)), dma((6,)), dma((6,)), dma((4,)), dma((4,)), dma((2,))]
    step = pl.pallas_call(
        kernel,
        out_shape=outs,
        in_specs=[any_] * 4 + [pl.BlockSpec(memory_space=VMEM)],
        out_specs=[any_] * len(outs),
        scratch_shapes=scratch,
        compiler_params=pltpu.CompilerParams(collective_id=0, has_side_effects=True, vmem_limit_bytes=63 << 20),
        name="step",
    )

    def body(x, dy, wg, wu, wd):
        by_g, by_u, by_d, dx = step(x[0], dy[0], wg, wu, wd)[:4]
        return dx[None], by_g, by_u, by_d

    seq, rows = P(("rep", "dp"), None, None), P(None, "dp", None)
    out = P("rep", "dp", None)
    return jax.shard_map(body, mesh=mesh, in_specs=(seq, seq, rows, rows, rows), out_specs=(seq, out, out, out), check_vma=False)
```

time: 800 us -> 445 us (0.56)
  Pallas kernels: 0 us -> 432 us
  matrix products: 342 us -> 0 us
  waiting for transfers between devices: 313 us -> 0 us
  other arithmetic: 85.2 us -> 0 us
  local copies, waits for them, and re-layouts: 37.6 us -> 8.11 us
  between operations: 14.9 us -> 0.66 us
    pallas_call x0 -> x1, Pallas kernels: none -> 432 us  [body(): by_g, by_u, by_d, dx = step(x[0], dy[0], wg, wu, wd)[:4]]
    dot_general x17 -> x0, matrix products: 342 us -> none  [the longest x6 128 us: layer(): up = jnp.dot(a, w['w_up'], preferred_element_type=jnp.float32)]
    unnamed x18 -> x0, waiting for transfers between devices: 237 us -> none
    squeeze x6 -> x0, waiting for transfers between devices: 76.3 us -> none  [stack(): h = layer(h, {name: w[number] for name, w in weights.items()})]
    unnamed x3 -> x0, other arithmetic: 62.6 us -> none
    unnamed x37 -> x10, local copies, waits for them, and re-layouts: 30 us -> 8.11 us
    add_any x2 -> x0, other arithmetic: 9.4 us -> none  [normed(): wide = h.astype(jnp.float32)]
    broadcast_in_dim x6 -> x0, other arithmetic: 8.66 us -> none  [stack(): h = layer(h, {name: w[number] for name, w in weights.items()})]
  transfers between devices with their start and end apart: 12 -> 0, of which waited for: 7 -> 0; matrix products, arithmetic and copies ran while one was open for 57% -> 0% of each run, Pallas kernels for 0% -> 0%
where the time goes in v2:
time: 445 us; the launch traced here: 441 us
  Pallas kernels  432 us (97%)
  local copies, waits for them, and re-layouts  8.11 us (2%)
    pallas_call x1, Pallas kernels, body(): by_g, by_u, by_d, dx = step(x[0], dy[0], wg, wu, wd)[:4]  432 us

profile of v2, /device:TPU:0, one launch (start us, length us, event | category | flops | bytes accessed | tf_op | source)
XLA Modules:
  0.0 441.0 jit_solution(9691171869854228131)
XLA Ops:
  0.6 432.2 %step.1 = (bf16[2,128,2816]{2,1,0:T(8,128)(2,1)}, bf16[2,128,2816]{2,1,0:T(8,128)(2,1)}, bf16[2,352,1024]{2,1,0:T(8,128)(2,1)}, bf16[2048,1024]{1,0:T(8,128)(2,1...) custom-call(bf16[2048,1024]{1,0:T(8,128)(2,1)} %bitcast.3, ...), custom_call_target="tpu_custom_call" | custom-call | tf_op jit(solution)/shard_map/step/pallas_call | solution.py:523
  432.9 0.0 copy-start.2
  432.9 0.0 copy-start.1
  432.9 4.8 %copy.13 = bf16[1,2048,1024]{2,1,0:T(8,128)(2,1)} copy(bf16[1,2048,1024]{2,1,0:T(8,128)(2,1)} %bitcast.5) | data formatting | bytes 8388608
  437.7 0.0 copy-done.2
  437.7 0.0 copy-start
  437.7 1.1 copy.14
  438.8 0.0 copy-done.1
  438.8 1.1 copy.15
  439.9 0.0 copy-done
  439.9 1.1 copy.16
Async XLA Ops:
  432.9 4.8 %copy-start.2 = (bf16[2,128,2816]{2,1,0:T(8,128)(2,1)S(1)}, bf16[2,128,2816]{2,1,0:T(8,128)(2,1)}, u32[]{:S(2)}) copy-start(bf16[2,128,2816]{2,1,0:T(8,128)(2,1)} %get-tuple-element.17) | copy-start | bytes 4325380
  432.9 5.9 %copy-start.1 = (bf16[2,128,2816]{2,1,0:T(8,128)(2,1)S(1)}, bf16[2,128,2816]{2,1,0:T(8,128)(2,1)}, u32[]{:S(2)}) copy-start(bf16[2,128,2816]{2,1,0:T(8,128)(2,1)} %get-tuple-element.18) | copy-start | bytes 4325380
  437.7 2.2 copy-start

commit v3 on v2

--- a/solution.py
+++ b/solution.py
@@ -60,6 +60,10 @@
     return pl.BlockSpec((rows, cols), index)
 
 
+def deep(rows, cols, index):
+    return pl.BlockSpec((rows, cols), index, pipeline_mode=pl.Buffered(3))
+
+
 def row(i):
     return i, 0
 
@@ -88,7 +92,7 @@
     (by_g, by_u, by_d, dx), refs = refs[:4], refs[4:]
     full, term, from_peer, refs = refs[:6], refs[6:12], refs[12:18], refs[18:]
     a0, a0t, h1, a1, a1t, act0, gu0, act1, dgu1, dact1, dh1, dgu0, refs = *refs[:12], refs[12:]
-    weights, down, resident, resident_t, *landings, gsend, dsend, gload, dload, gsem, gsem2, send, recv, local, mix, extra, lsem, osem = refs
+    weights, resident, resident_t, *landings, gsend, dsend, gload, dload, gsem, gsem2, send, recv, local, mix, extra, lsem, osem = refs
     me, flip = places()
     nx, ny, peer, nxy = flip(1, 0, 0), flip(0, 1, 0), flip(0, 0, 1), flip(1, 1, 0)
     shards = [wd.at[n] if part == 2 else gload.at[2 * n + part] for n, part in UNITS]
@@ -325,12 +329,21 @@
                 act_ref[m : m + M, :] = (g * sigmoid(g) * up).astype(BF)
 
         cols = lambda j: (0, j + STEPS * half)
-        pipeline(body, (STEPS,), [block(D, W, col)], [block(T, W, cols), block(T, L, cols)], None, full[half], gu0, act0)
-
-    def down_body(act_ref, x_ref, h_ref, a_ref, at_ref):
-        h = x_ref[...] + dot(act_ref[...], down[...]).astype(BF)
-        h_ref[...] = h
-        norm_into(h.astype(F32), a_ref, at_ref)
+        tiles = pl.BlockSpec((None, T, W), lambda j: (j + STEPS * half, 0, 0))
+        pipeline(body, (STEPS,), [block(D, W, col)], [tiles, block(T, L, cols)], None, full[half], gu0, act0)
+
+    def down_op(down, sem):
+        in_down = pltpu.make_async_copy(full[2], down, sem)
+        in_down.start()
+        in_down.wait()
+
+        def body(act_ref, x_ref, h_ref, a_ref, at_ref):
+            h = x_ref[...] + dot(act_ref[...], down[...]).astype(BF)
+            h_ref[...] = h
+            norm_into(h.astype(F32), a_ref, at_ref)
+
+        outs = [block(M, D, row), block(M, D, row), block(D, M, col)]
+        pipeline(body, (T // M,), [block(M, FF, row), block(M, D, row)], outs, None, act0, x, h1, a1, a1t)
 
     def dact_body(w_ref, out_ref):
         for m in range(0, T, M):
@@ -363,14 +376,14 @@
             for m in range(0, D, M):
                 out_ref[m : m + M, :] = dot(resident_t[m : m + M, :], d_ref[...]).astype(BF)
 
-        pipeline(body, (STEPS,), [block(T, W, lambda j: (0, j + STEPS * half))], [block(D, W, col)], hooks, dgu, term[u])
+        pipeline(body, (STEPS,), [deep(T, W, lambda j: (0, j + STEPS * half))], [block(D, W, col)], hooks, dgu, term[u])
         send_term(u)
 
     def grad_down(u, act, hooks):
         def body(act_ref, out_ref):
             out_ref[...] = dotg(act_ref[...], resident[...], TN).astype(BF)
 
-        pipeline(body, (STEPS,), [block(T, W, col)], [block(W, D, row)], hooks, act, term[u])
+        pipeline(body, (STEPS,), [deep(T, W, col)], [block(W, D, row)], hooks, act, term[u])
         send_term(u)
 
     def grad_in(dgu, h, dh, out, keep, hooks):
@@ -387,20 +400,23 @@
 
         pipeline(body, (T // W,), [block(W, 2 * FF, row)] + [block(W, D, row)] * 2, [block(W, D, row)], hooks, dgu, h, dh, out)
 
-    def act_back(hooks):
-        def body(w_ref, gu_ref, dgu_ref):
-            first = pl.program_id(0) * (T // 2)
-            for m in range(0, T // 2, M):
+    def act_back(u, hooks):
+        def body(w_ref, gu_ref, dgu_ref, out_ref):
+            for m in range(0, T, M):
                 rows = slice(m, m + M)
-                dd = dotg(resident[pl.ds(pl.multiple_of(first + m, M), M), :], w_ref[...], NT).astype(BF).astype(F32)
+                dd = dotg(resident[rows, :], w_ref[...], NT).astype(BF).astype(F32)
                 for n in range(2):
-                    at = W * n
-                    _, dg, du = back(gu_ref[rows, at : at + L], gu_ref[rows, at + L : at + W], dd[:, L * n : L * n + L])
+                    at, up = W * n, gu_ref[n, rows, L:]
+                    silu, dg, du = back(gu_ref[n, rows, :L], up, dd[:, L * n : L * n + L])
                     dgu_ref[rows, at : at + L] = dg
                     dgu_ref[rows, at + L : at + W] = du
-
-        wide = block(T // 2, M, lambda i, j: (i, j))
-        pipeline(body, (2, STEPS), [block(W, D, lambda i, j: (j, 0)), wide], [wide], hooks, full[2], gu0, dgu0)
+                    weights[m // D, m % D : m % D + M, L * n : L * n + L] = (silu * up).astype(BF)
+            low, high = (dotg(weights[i, :, :W], resident[D * i : D * i + D, :], TN) for i in range(2))
+            out_ref[...] = (low + high).astype(BF)
+
+        tiles = pl.BlockSpec((2, T, W), lambda j: (j, 0, 0))
+        pipeline(body, (STEPS,), [block(W, D, row), tiles], [block(T, M, col), block(W, D, row)], hooks, full[2], gu0, dgu0, term[u])
+        send_term(u)
 
     for u in (0, 1, 4, 5):
         mix_start(u)
@@ -432,11 +448,7 @@
     pass_on(3)
     start_own(5)
     arrived(2)
-    in_down = load(full[2], down, 1)
-    in_down.start()
-    in_down.wait()
-    outs = [block(M, D, row), block(M, D, row), block(D, M, col)]
-    pipeline(down_body, (T // M,), [block(M, FF, row), block(M, D, row)], outs, None, act0, x, h1, a1, a1t)
+    pl.run_scoped(down_op, VMEM((FF, D), BF), pltpu.SemaphoreType.DMA)
     in_at = load(a1t, resident_t, 1)
     in_at.start()
     in_dy.wait()
@@ -471,18 +483,17 @@
     for c in in_w:
         c.wait()
     grad_in(dgu1, h1, dy, dh1, True, {0: fetch2(5), 1: together(pass2(5), fetch1(3)), 3: pass1(3), 6: fetch3(5), 7: pass3(5)})
+    act_back(2, {0: fetch2(3), 1: pass2(3), 6: fetch3(3), 7: pass3(3)})
     in_w = [load(full[i], weights.at[i], 2 + i) for i in range(2)]
     for c in in_w:
         c.start()
-    grad_down(2, act0, {0: fetch2(3), 2: pass2(3)})
-    act_back({4: fetch3(3), 7: together(pass3(3), fetch1(2)), 10: pass1(2)})
     in_at.wait()
-    grad_gu(0, dgu0, {0: fetch2(2), 2: pass2(2)})
-    grad_gu(1, dgu0, {4: fetch1(0), 6: pass1(0), 7: fetch3(2), 10: pass3(2)})
+    grad_gu(0, dgu0, {4: fetch1(2), 6: pass1(2)})
+    grad_gu(1, dgu0, {1: fetch2(2), 3: pass2(2), 5: fetch1(0), 7: pass1(0)})
     for c in in_w:
         c.wait()
-    grad_in(dgu0, x, dh1, dx, False, {0: fetch2(0), 1: together(pass2(0), fetch1(1)), 2: pass1(1), 6: fetch3(0), 7: together(pass3(0), fetch2(1))})
-    pass2(1)()
+    grad_in(dgu0, x, dh1, dx, False, {1: fetch1(1), 2: together(pass1(1), fetch2(0)), 3: together(pass2(0), fetch3(2)), 4: pass3(2), 6: fetch2(1), 7: together(pass2(1), fetch3(0))})
+    pass3(0)()
     fetch3(1)()
     pass3(1)()
     for u in (1, 2):
@@ -503,8 +514,8 @@
     outs = [s(2, GROWS, FF), s(2, GROWS, FF), s(2, DROWS, D), s(T, D)]
     outs += [s(*full_shape(u)) for u in range(6)] * 2
     outs += [s(4 * rows_of(u), full_shape(u)[1]) for u in range(6)]
-    outs += [s(T, D), s(D, T), s(T, D), s(T, D), s(D, T), s(T, FF), s(T, 2 * FF, dtype=F32), s(T, FF), s(T, 2 * FF), s(T, FF), s(T, D), s(T, 2 * FF)]
-    scratch = [VMEM((2, D, FF), BF), VMEM((FF, D), BF), VMEM((T, D), BF), VMEM((D, T), BF)]
+    outs += [s(T, D), s(D, T), s(T, D), s(T, D), s(D, T), s(T, FF), s(2 * STEPS, T, W, dtype=F32), s(T, FF), s(T, 2 * FF), s(T, FF), s(T, D), s(T, 2 * FF)]
+    scratch = [VMEM((2, D, FF), BF), VMEM((T, D), BF), VMEM((D, T), BF)]
     scratch += [VMEM((4, r, FF), BF) for r in (GROWS // 2, GROWS // 2, GROWS, GROWS)]
     scratch += [VMEM((2, r, D), BF) for r in (DROWS // 2, DROWS // 2, DROWS, DROWS)]
     scratch += [VMEM((3, GROWS, FF), BF), VMEM((3, DROWS, D), BF), VMEM((4, GROWS, FF), BF), VMEM((4, DROWS, D), BF)]

time: 445 us -> 425 us (0.955)
  Pallas kernels: 432 us -> 414 us
    pallas_call x1, Pallas kernels: 432 us -> 414 us  [body(): by_g, by_u, by_d, dx = step(x[0], dy[0], wg, wu, wd)[:4]]
where the time goes in v3:
time: 425 us; the launch traced here: 423 us
  Pallas kernels  414 us (97%)
  local copies, waits for them, and re-layouts  8.11 us (2%)
    pallas_call x1, Pallas kernels, body(): by_g, by_u, by_d, dx = step(x[0], dy[0], wg, wu, wd)[:4]  414 us

profile of v3, /device:TPU:0, one launch (start us, length us, event | category | flops | bytes accessed | tf_op | source)
XLA Modules:
  0.0 422.7 jit_solution(6699106298944403637)
XLA Ops:
  0.6 414.0 %step.1 = (bf16[2,128,2816]{2,1,0:T(8,128)(2,1)}, bf16[2,128,2816]{2,1,0:T(8,128)(2,1)}, bf16[2,352,1024]{2,1,0:T(8,128)(2,1)}, bf16[2048,1024]{1,0:T(8,128)(2,1...) custom-call(bf16[2048,1024]{1,0:T(8,128)(2,1)} %bitcast.3, ...), custom_call_target="tpu_custom_call" | custom-call | tf_op jit(solution)/shard_map/step/pallas_call | solution.py:534
  414.6 0.0 copy-start.2
  414.6 0.0 copy-start.1
  414.6 4.8 %copy.13 = bf16[1,2048,1024]{2,1,0:T(8,128)(2,1)} copy(bf16[1,2048,1024]{2,1,0:T(8,128)(2,1)} %bitcast.5) | data formatting | bytes 8388608
  419.4 0.0 copy-done.2
  419.4 0.0 copy-start
  419.4 1.1 copy.14
  420.5 0.0 copy-done.1
  420.5 1.1 copy.15
  421.6 0.0 copy-done
  421.6 1.1 copy.16
Async XLA Ops:
  414.6 4.8 %copy-start.2 = (bf16[2,128,2816]{2,1,0:T(8,128)(2,1)S(1)}, bf16[2,128,2816]{2,1,0:T(8,128)(2,1)}, u32[]{:S(2)}) copy-start(bf16[2,128,2816]{2,1,0:T(8,128)(2,1)} %get-tuple-element.17) | copy-start | bytes 4325380
  414.6 5.9 %copy-start.1 = (bf16[2,128,2816]{2,1,0:T(8,128)(2,1)S(1)}, bf16[2,128,2816]{2,1,0:T(8,128)(2,1)}, u32[]{:S(2)}) copy-start(bf16[2,128,2816]{2,1,0:T(8,128)(2,1)} %get-tuple-element.18) | copy-start | bytes 4325380
  419.4 2.2 copy-start

commit v4 on v3

--- a/solution.py
+++ b/solution.py
@@ -90,15 +90,18 @@
 
 def kernel(x, dy, wg, wu, wd, *refs):
     (by_g, by_u, by_d, dx), refs = refs[:4], refs[4:]
-    full, term, from_peer, refs = refs[:6], refs[6:12], refs[12:18], refs[18:]
+    full, term_gu, term_d, from_peer, refs = refs[:6], refs[6:8], refs[8:10], refs[10:16], refs[16:]
     a0, a0t, h1, a1, a1t, act0, gu0, act1, dgu1, dact1, dh1, dgu0, refs = *refs[:12], refs[12:]
     weights, resident, resident_t, *landings, gsend, dsend, gload, dload, gsem, gsem2, send, recv, local, mix, extra, lsem, osem = refs
     me, flip = places()
     nx, ny, peer, nxy = flip(1, 0, 0), flip(0, 1, 0), flip(0, 0, 1), flip(1, 1, 0)
-    shards = [wd.at[n] if part == 2 else gload.at[2 * n + part] for n, part in UNITS]
+    shards = [wd.at[n] if half == 2 else gload.at[2 * n + half] for n, half in UNITS]
 
     def load(src, dst, n):
         return pltpu.make_async_copy(src, dst, extra.at[n])
+
+    def kind(u):
+        return UNITS[u][1] == 2
 
 
     def part(u, b, half=None):
@@ -107,33 +110,50 @@
             return full[u].at[pl.ds(b * r, r), :]
         return full[u].at[pl.ds(b * r + half * (r // 2), r // 2), :]
 
+    def piece(u):
+        return 96 if kind(u) else 32
+
     def hop(u, k):
+        r, p = rows_of(u), piece(u)
+        low, high = pl.ds(0, p), pl.ds(p, r - p)
+        mine = part(u, me)
         src, dst, to = (
-            (shards[u], part(u, me), nx),
-            (shards[u], part(u, me), ny),
-            (shards[u], part(u, me), peer),
+            (shards[u].at[high, :], mine.at[high, :], nx),
+            (shards[u].at[high, :], mine.at[high, :], ny),
+            (shards[u], mine, peer),
             (part(u, nx, 0), part(u, nx, 0), ny),
             (part(u, ny, 1), part(u, ny, 1), nx),
             (part(u, nx), part(u, nx), peer),
             (part(u, ny), part(u, ny), peer),
             (part(u, nxy, 0), part(u, nxy, 0), peer),
             (part(u, nxy, 1), part(u, nxy, 1), peer),
+            (shards[u].at[low, :], mine.at[low, :], nx),
+            (shards[u].at[low, :], mine.at[low, :], ny),
         )[k]
         return remote(src, dst, gsem.at[u, k], gsem2.at[u, k], to)
 
     def own_copy(u):
         return pltpu.make_async_copy(shards[u], part(u, me), local.at[u])
 
-    def start_own(u):
+    def start_first(u):
+        hop(u, 9).start()
+        hop(u, 10).start()
+
+    def start_rest(u):
         for k in range(3):
             hop(u, k).start()
         own_copy(u).start()
 
     def pass_on(u):
         for k in (0, 1):
+            hop(u, k + 9).wait_recv()
             hop(u, k).wait_recv()
             hop(u, k + 3).start()
             hop(u, k + 5).start()
+        if u < 5:
+            start_rest(u + 1)
+        if u < 4:
+            start_first(u + 2)
 
     def pass_on_last(u):
         for k in (3, 4):
@@ -157,9 +177,6 @@
 
     where = (me, nx, ny, nxy)
 
-    def kind(u):
-        return UNITS[u][1] == 2
-
     slot = (0, 1, 0, 1, 2, 3)
     before = {5: 4, 0: 5, 1: 0, 2: 3}
 
@@ -171,13 +188,18 @@
 
     def loading(u):
         return dload if kind(u) else gload
+
+    def term(u, b):
+        n, half = UNITS[u]
+        rows = pl.ds(b * rows_of(u), rows_of(u))
+        return term_d[n].at[rows, :] if half == 2 else term_gu[n].at[rows, pl.ds(half * FF, FF)]
 
     def copy(u, k):
         r = rows_of(u)
         if k < 4:
             b = where[k]
             other = b + 1 - 2 * (b % 2)
-            return remote(term[u].at[pl.ds(other * r, r), :], from_peer[u].at[pl.ds((b // 2) * r, r), :], send.at[u, k], recv.at[u, k], peer)
+            return remote(term(u, other), from_peer[u].at[pl.ds((b // 2) * r, r), :], send.at[u, k], recv.at[u, k], peer)
         s, (l1x, l1y, l2x, l2y) = sending(u), landing(u)
         half = r // 2
         src, dst, to = (
@@ -196,7 +218,7 @@
         r, v = rows_of(u), loading(u)
         for n, q in enumerate(qs):
             b = where[q]
-            yield pltpu.make_async_copy(term[u].at[pl.ds(b * r, r), :], v.at[n], lsem.at[2 * n])
+            yield pltpu.make_async_copy(term(u, b), v.at[n], lsem.at[2 * n])
             yield pltpu.make_async_copy(from_peer[u].at[pl.ds((b // 2) * r, r), :], v.at[n + 2], lsem.at[2 * n + 1])
 
     def fetch(u, *qs):
@@ -320,7 +342,7 @@
     def norm_body(x_ref, a_ref, at_ref):
         norm_into(x_ref[...].astype(F32), a_ref, at_ref)
 
-    def gate_up0(half):
+    def gate_up0(half, hooks):
         def body(w_ref, gu_ref, act_ref):
             for m in range(0, T, M):
                 s = dot(resident[m : m + M, :], w_ref[...])
@@ -330,7 +352,7 @@
 
         cols = lambda j: (0, j + STEPS * half)
         tiles = pl.BlockSpec((None, T, W), lambda j: (j + STEPS * half, 0, 0))
-        pipeline(body, (STEPS,), [block(D, W, col)], [tiles, block(T, L, cols)], None, full[half], gu0, act0)
+        pipeline(body, (STEPS,), [block(D, W, col)], [tiles, block(T, L, cols)], hooks, full[half], gu0, act0)
 
     def down_op(down, sem):
         in_down = pltpu.make_async_copy(full[2], down, sem)
@@ -343,7 +365,7 @@
             norm_into(h.astype(F32), a_ref, at_ref)
 
         outs = [block(M, D, row), block(M, D, row), block(D, M, col)]
-        pipeline(body, (T // M,), [block(M, FF, row), block(M, D, row)], outs, None, act0, x, h1, a1, a1t)
+        pipeline(body, (T // M,), [block(M, FF, row), block(M, D, row)], outs, {2: lambda: pass_on(3)}, act0, x, h1, a1, a1t)
 
     def dact_body(w_ref, out_ref):
         for m in range(0, T, M):
@@ -369,21 +391,20 @@
         ins, outs = [block(D, W, col), block(T, L, cols)], [block(T, L, cols), block(T, W, cols)]
         pipeline(body, (STEPS,), ins, outs, hooks, full[4 + half], dact1, act1, dgu1)
 
-    def grad_gu(u, dgu, hooks):
-        half = UNITS[u][1]
-
+    def grad_gu(n, first, second, dgu, hooks):
         def body(d_ref, out_ref):
             for m in range(0, D, M):
                 out_ref[m : m + M, :] = dot(resident_t[m : m + M, :], d_ref[...]).astype(BF)
 
-        pipeline(body, (STEPS,), [deep(T, W, lambda j: (0, j + STEPS * half))], [block(D, W, col)], hooks, dgu, term[u])
-        send_term(u)
+        early = {7: together(*hooks.pop(7, ()), lambda: send_term(first))}
+        pipeline(body, (STEPS,), [deep(T, M, col)], [block(D, M, col)], hooks | early, dgu, term_gu[n])
+        send_term(second)
 
     def grad_down(u, act, hooks):
         def body(act_ref, out_ref):
             out_ref[...] = dotg(act_ref[...], resident[...], TN).astype(BF)
 
-        pipeline(body, (STEPS,), [deep(T, W, col)], [block(W, D, row)], hooks, act, term[u])
+        pipeline(body, (STEPS,), [deep(T, W, col)], [block(W, D, row)], hooks, act, term_d[UNITS[u][0]])
         send_term(u)
 
     def grad_in(dgu, h, dh, out, keep, hooks):
@@ -415,84 +436,76 @@
             out_ref[...] = (low + high).astype(BF)
 
         tiles = pl.BlockSpec((2, T, W), lambda j: (j, 0, 0))
-        pipeline(body, (STEPS,), [block(W, D, row), tiles], [block(T, M, col), block(W, D, row)], hooks, full[2], gu0, dgu0, term[u])
+        pipeline(body, (STEPS,), [block(W, D, row), tiles], [block(T, M, col), block(W, D, row)], hooks, full[2], gu0, dgu0, term_d[0])
         send_term(u)
 
     for u in (0, 1, 4, 5):
         mix_start(u)
     barrier((nx, ny, peer))
-    for u in range(2):
-        mix_wait(u)
-        start_own(u)
+    mix_wait(0)
+    start_first(0)
+    start_rest(0)
+    mix_wait(1)
+    start_first(1)
     mix_wait(4)
     mix_wait(5)
     pipeline(norm_body, (T // W,), [block(W, D, row)], [block(W, D, row), block(D, W, col)], None, x, a0, a0t)
     in_a = load(a0, resident, 0)
     in_a.start()
     pass_on(0)
-    start_own(2)
     pass_on_last(0)
-    pass_on(1)
-    start_own(3)
+    in_a.wait()
     arrived(0)
-    in_a.wait()
-    gate_up0(0)
+    gate_up0(0, {6: lambda: pass_on(1)})
     pass_on_last(1)
-    pass_on(2)
-    start_own(4)
     arrived(1)
-    gate_up0(1)
+    gate_up0(1, {6: lambda: pass_on(2)})
     in_dy = load(dy, resident, 0)
     in_dy.start()
     pass_on_last(2)
-    pass_on(3)
-    start_own(5)
     arrived(2)
     pl.run_scoped(down_op, VMEM((FF, D), BF), pltpu.SemaphoreType.DMA)
     in_at = load(a1t, resident_t, 1)
     in_at.start()
     in_dy.wait()
     pass_on_last(3)
-    pass_on(4)
     arrived(3)
-    pipeline(dact_body, (STEPS,), [block(W, D, row)], [block(T, W, col)], None, full[3], dact1)
+    pipeline(dact_body, (STEPS,), [block(W, D, row)], [block(T, W, col)], {6: lambda: pass_on(4)}, full[3], dact1)
     in_a = load(a1, resident, 0)
     in_a.start()
     pass_on_last(4)
     in_at.wait()
     in_a.wait()
     arrived(4)
-    gate_up1(0, {5: lambda: pass_on(5)})
-    grad_gu(4, dgu1, None)
+    gate_up1(0, {6: lambda: pass_on(5)})
     pass_on_last(5)
     arrived(5)
-    for u in range(6):
-        for k in range(9):
-            hop(u, k).wait_send()
     in_w = [load(full[4 + i], weights.at[i], 2 + i) for i in range(2)]
     for c in in_w:
         c.start()
-    gate_up1(1, {4: fetch1(4), 6: pass1(4)})
+    gate_up1(1, None)
+    for u in range(6):
+        for k in range(11):
+            hop(u, k).wait_send()
     in_dy = load(dy, resident, 0)
     in_dy.start()
-    grad_gu(5, dgu1, {1: fetch2(4), 4: pass2(4)})
+    grad_gu(1, 4, 5, dgu1, {})
     in_at = load(a0t, resident_t, 1)
     in_at.start()
     in_dy.wait()
-    grad_down(3, act1, {4: fetch1(5), 6: pass1(5), 7: fetch3(4), 9: pass3(4)})
+    grad_down(3, act1, {0: fetch1(4), 2: together(pass1(4), fetch1(5)), 5: pass1(5), 8: fetch2(4), 10: pass2(4)})
     for c in in_w:
         c.wait()
-    grad_in(dgu1, h1, dy, dh1, True, {0: fetch2(5), 1: together(pass2(5), fetch1(3)), 3: pass1(3), 6: fetch3(5), 7: pass3(5)})
-    act_back(2, {0: fetch2(3), 1: pass2(3), 6: fetch3(3), 7: pass3(3)})
+    grad_in(dgu1, h1, dy, dh1, True, {1: fetch2(5), 2: together(pass2(5), fetch1(3)), 3: pass1(3), 6: fetch3(4), 7: pass3(4)})
+    act_back(2, {1: fetch3(5), 2: pass3(5), 3: fetch2(3), 4: pass2(3), 9: fetch3(3), 10: pass3(3)})
     in_w = [load(full[i], weights.at[i], 2 + i) for i in range(2)]
     for c in in_w:
         c.start()
     in_at.wait()
-    grad_gu(0, dgu0, {4: fetch1(2), 6: pass1(2)})
-    grad_gu(1, dgu0, {1: fetch2(2), 3: pass2(2), 5: fetch1(0), 7: pass1(0)})
+    grad_gu(0, 0, 1, dgu0, {2: fetch1(2), 3: pass1(2), 6: fetch2(2), 7: (pass2(2),), 10: fetch1(0)})
     for c in in_w:
         c.wait()
-    grad_in(dgu0, x, dh1, dx, False, {1: fetch1(1), 2: together(pass1(1), fetch2(0)), 3: together(pass2(0), fetch3(2)), 4: pass3(2), 6: fetch2(1), 7: together(pass2(1), fetch3(0))})
+    grad_in(dgu0, x, dh1, dx, False, {0: pass1(0), 1: fetch1(1), 2: together(pass1(1), fetch2(0)), 3: together(pass2(0), fetch3(2)), 4: pass3(2), 5: fetch2(1), 6: pass2(1), 7: fetch3(0)})
     pass3(0)()
     fetch3(1)()
     pass3(1)()
@@ -504,6 +517,20 @@
             copy(u, k).wait_send()
 
 
+def hand_on_kernel(*refs):
+    sources, targets, buffers, sems = refs[:4], refs[4:8], refs[8:12], refs[12]
+    arrays = range(4)
+    ins = [pltpu.make_async_copy(sources[i], buffers[i], sems.at[i]) for i in arrays]
+    outs = [pltpu.make_async_copy(buffers[i], targets[i], sems.at[4 + i]) for i in arrays]
+    for c in ins:
+        c.start()
+    for c, o in zip(ins, outs):
+        c.wait()
+        o.start()
+    for o in outs:
+        o.wait()
+
+
 def solution(mesh):
     any_ = pl.BlockSpec(memory_space=ANY)
     dma = pltpu.SemaphoreType.DMA
@@ -512,14 +539,15 @@
         return jax.ShapeDtypeStruct(shape, dtype)
 
     outs = [s(2, GROWS, FF), s(2, GROWS, FF), s(2, DROWS, D), s(T, D)]
-    outs += [s(*full_shape(u)) for u in range(6)] * 2
+    outs += [s(*full_shape(u)) for u in range(6)]
+    outs += [s(D, 2 * FF)] * 2 + [s(FF, D)] * 2
     outs += [s(4 * rows_of(u), full_shape(u)[1]) for u in range(6)]
     outs += [s(T, D), s(D, T), s(T, D), s(T, D), s(D, T), s(T, FF), s(2 * STEPS, T, W, dtype=F32), s(T, FF), s(T, 2 * FF), s(T, FF), s(T, D), s(T, 2 * FF)]
     scratch = [VMEM((2, D, FF), BF), VMEM((T, D), BF), VMEM((D, T), BF)]
     scratch += [VMEM((4, r, FF), BF) for r in (GROWS // 2, GROWS // 2, GROWS, GROWS)]
     scratch += [VMEM((2, r, D), BF) for r in (DROWS // 2, DROWS // 2, DROWS, DROWS)]
     scratch += [VMEM((3, GROWS, FF), BF), VMEM((3, DROWS, D), BF), VMEM((4, GROWS, FF), BF), VMEM((4, DROWS, D), BF)]
-    scratch += [dma((6, 9)), dma((6, 9)), dma((6, 8)), dma((6, 8)), dma((6,)), dma((6,)), dma((4,)), dma((4,)), dma((2,))]
+    scratch += [dma((6, 11)), dma((6, 11)), dma((6, 8)), dma((6, 8)), dma((6,)), dma((6,)), dma((4,)), dma((4,)), dma((2,))]
     step = pl.pallas_call(
         kernel,
         out_shape=outs,
@@ -530,8 +558,17 @@
         name="step",
     )
 
+    hand_on = pl.pallas_call(
+        hand_on_kernel,
+        out_shape=outs[:4],
+        in_specs=[any_] * 4,
+        out_specs=[any_] * 4,
+        scratch_shapes=[VMEM(o.shape, BF) for o in outs[:4]] + [dma((8,))],
+        name="hand_on",
+    )
+
     def body(x, dy, wg, wu, wd):
-        by_g, by_u, by_d, dx = step(x[0], dy[0], wg, wu, wd)[:4]
+        by_g, by_u, by_d, dx = hand_on(*step(x[0], dy[0], wg, wu, wd)[:4])
         return dx[None], by_g, by_u, by_d
 
     seq, rows = P(("rep", "dp"), None, None), P(None, "dp", None)

time: 425 us -> 414 us (0.974)
  local copies, waits for them, and re-layouts: 8.11 us -> 0 us
    unnamed x10 -> x0, local copies, waits for them, and re-layouts: 8.11 us -> none
    pallas_call x1 -> x2, Pallas kernels: 414 us -> 410 us  [body(): by_g, by_u, by_d, dx = hand_on(*step(x[0], dy[0], wg, wu, wd)[:4])]
where the time goes in v4:
time: 414 us; the launch traced here: 411 us
  Pallas kernels  410 us (99%)
    pallas_call x2, Pallas kernels, body(): by_g, by_u, by_d, dx = hand_on(*step(x[0], dy[0], wg, wu, wd)[:4])  410 us

profile of v4, /device:TPU:0, one launch (start us, length us, event | category | flops | bytes accessed | tf_op | source)
XLA Modules:
  0.0 411.1 jit_solution(10261986756334985207)
XLA Ops:
  0.6 403.2 %step.1 = (bf16[2,128,2816]{2,1,0:T(8,128)(2,1)}, bf16[2,128,2816]{2,1,0:T(8,128)(2,1)}, bf16[2,352,1024]{2,1,0:T(8,128)(2,1)}, bf16[2048,1024]{1,0:T(8,128)(2,1...) custom-call(bf16[2048,1024]{1,0:T(8,128)(2,1)} %bitcast.3, ...), custom_call_target="tpu_custom_call" | custom-call | tf_op jit(solution)/shard_map/step/pallas_call | solution.py:571
  403.8 7.2 %hand_on.1 = (bf16[2,128,2816]{2,1,0:T(8,128)(2,1)}, bf16[2,128,2816]{2,1,0:T(8,128)(2,1)}, bf16[2,352,1024]{2,1,0:T(8,128)(2,1)}, bf16[2048,1024]{1,0:T(8,128)(2,1)}) custom-call(bf16[2,128,2816]{2,1,0:T(8,128)(2,1)} %get-tuple-element.12.refs_0_, bf16[2,128,2816]{2,1,0:T(8,128)(2,1)} %get-tuple-element.13.refs_1_, ...), custom_call_target="tpu_custom_call" | custom-call | tf_op jit(solution)/shard_map/hand_on/pallas_call | solution.py:571

commit v5 on v4

--- a/solution.py
+++ b/solution.py
@@ -91,7 +91,7 @@
 def kernel(x, dy, wg, wu, wd, *refs):
     (by_g, by_u, by_d, dx), refs = refs[:4], refs[4:]
     full, term_gu, term_d, from_peer, refs = refs[:6], refs[6:8], refs[8:10], refs[10:16], refs[16:]
-    a0, a0t, h1, a1, a1t, act0, gu0, act1, dgu1, dact1, dh1, dgu0, refs = *refs[:12], refs[12:]
+    a0, a0t, h1, a1, a1t, act0, gu0, dgu1, dact1, dh1, dgu0, refs = *refs[:11], refs[11:]
     weights, resident, resident_t, *landings, gsend, dsend, gload, dload, gsem, gsem2, send, recv, local, mix, extra, lsem, osem = refs
     me, flip = places()
     nx, ny, peer, nxy = flip(1, 0, 0), flip(0, 1, 0), flip(0, 0, 1), flip(1, 1, 0)
@@ -377,19 +377,21 @@
         return silu, (d * up * (sg + silu * (1.0 - sg))).astype(BF), (d * silu).astype(BF)
 
     def gate_up1(half, hooks):
-        def body(w_ref, dact_ref, act_ref, dgu_ref):
+        def body(w_ref, dact_ref, dgu_ref, out_ref):
             for m in range(0, T, M):
                 rows = slice(m, m + M)
                 s = dot(resident[rows, :], w_ref[...])
                 up = s[:, L:]
                 silu, dg, du = back(s[:, :L], up, dact_ref[rows, :].astype(F32))
-                act_ref[rows, :] = (silu * up).astype(BF)
+                weights[m // D, m % D : m % D + M, D : D + L] = (silu * up).astype(BF)
                 dgu_ref[rows, :L] = dg
                 dgu_ref[rows, L:] = du
+            low, high = (dotg(weights[i, :, D : D + L], weights[i, :, :D], TN) for i in range(2))
+            out_ref[...] = (low + high).astype(BF)
 
         cols = lambda j: (0, j + STEPS * half)
-        ins, outs = [block(D, W, col), block(T, L, cols)], [block(T, L, cols), block(T, W, cols)]
-        pipeline(body, (STEPS,), ins, outs, hooks, full[4 + half], dact1, act1, dgu1)
+        ins, outs = [block(D, W, col), block(T, L, cols)], [block(T, W, cols), block(L, D, lambda j: (j + STEPS * half, 0))]
+        pipeline(body, (STEPS,), ins, outs, hooks, full[4 + half], dact1, dgu1, term_d[1])
 
     def grad_gu(n, first, second, dgu, hooks):
         def body(d_ref, out_ref):
@@ -399,13 +401,6 @@
         early = {7: together(*hooks.pop(7, ()), lambda: send_term(first))}
         pipeline(body, (STEPS,), [deep(T, M, col)], [block(D, M, col)], hooks | early, dgu, term_gu[n])
         send_term(second)
-
-    def grad_down(u, act, hooks):
-        def body(act_ref, out_ref):
-            out_ref[...] = dotg(act_ref[...], resident[...], TN).astype(BF)
-
-        pipeline(body, (STEPS,), [deep(T, W, col)], [block(W, D, row)], hooks, act, term_d[UNITS[u][0]])
-        send_term(u)
 
     def grad_in(dgu, h, dh, out, keep, hooks):
         def body(d_ref, h_ref, dh_ref, out_ref):
@@ -423,15 +418,15 @@
 
     def act_back(u, hooks):
         def body(w_ref, gu_ref, dgu_ref, out_ref):
-            for m in range(0, T, M):
-                rows = slice(m, m + M)
+            for m in range(0, T, W):
+                rows = slice(m, m + W)
                 dd = dotg(resident[rows, :], w_ref[...], NT).astype(BF).astype(F32)
                 for n in range(2):
                     at, up = W * n, gu_ref[n, rows, L:]
                     silu, dg, du = back(gu_ref[n, rows, :L], up, dd[:, L * n : L * n + L])
                     dgu_ref[rows, at : at + L] = dg
                     dgu_ref[rows, at + L : at + W] = du
-                    weights[m // D, m % D : m % D + M, L * n : L * n + L] = (silu * up).astype(BF)
+                    weights[m // D, m % D : m % D + W, L * n : L * n + L] = (silu * up).astype(BF)
             low, high = (dotg(weights[i, :, :W], resident[D * i : D * i + D, :], TN) for i in range(2))
             out_ref[...] = (low + high).astype(BF)
 
@@ -473,31 +468,33 @@
     pipeline(dact_body, (STEPS,), [block(W, D, row)], [block(T, W, col)], {6: lambda: pass_on(4)}, full[3], dact1)
     in_a = load(a1, resident, 0)
     in_a.start()
+    in_dy = [load(dy.at[pl.ds(D * i, D), :], weights.at[i, :, pl.ds(0, D)], 2 + i) for i in range(2)]
+    for c in in_dy:
+        c.start()
     pass_on_last(4)
     in_at.wait()
     in_a.wait()
+    for c in in_dy:
+        c.wait()
     arrived(4)
     gate_up1(0, {6: lambda: pass_on(5)})
     pass_on_last(5)
     arrived(5)
+    gate_up1(1, None)
+    send_term(3)
     in_w = [load(full[4 + i], weights.at[i], 2 + i) for i in range(2)]
     for c in in_w:
         c.start()
-    gate_up1(1, None)
     for u in range(6):
         for k in range(11):
             hop(u, k).wait_send()
-    in_dy = load(dy, resident, 0)
-    in_dy.start()
-    grad_gu(1, 4, 5, dgu1, {})
+    grad_gu(1, 4, 5, dgu1, {3: fetch1(3), 4: pass1(3), 8: fetch2(3), 9: pass2(3)})
     in_at = load(a0t, resident_t, 1)
     in_at.start()
-    in_dy.wait()
-    grad_down(3, act1, {0: fetch1(4), 2: together(pass1(4), fetch1(5)), 5: pass1(5), 8: fetch2(4), 10: pass2(4)})
     for c in in_w:
         c.wait()
-    grad_in(dgu1, h1, dy, dh1, True, {1: fetch2(5), 2: together(pass2(5), fetch1(3)), 3: pass1(3), 6: fetch3(4), 7: pass3(4)})
-    act_back(2, {1: fetch3(5), 2: pass3(5), 3: fetch2(3), 4: pass2(3), 9: fetch3(3), 10: pass3(3)})
+    grad_in(dgu1, h1, dy, dh1, True, {0: fetch1(4), 1: together(pass1(4), fetch1(5)), 2: pass1(5), 3: fetch2(4), 4: together(pass2(4), fetch3(3)), 5: together(pass3(3), fetch2(5)), 6: pass2(5)})
+    act_back(2, {3: fetch3(4), 4: pass3(4), 8: fetch3(5), 9: pass3(5)})
     in_w = [load(full[i], weights.at[i], 2 + i) for i in range(2)]
     for c in in_w:
         c.start()
@@ -542,7 +539,7 @@
     outs += [s(*full_shape(u)) for u in range(6)]
     outs += [s(D, 2 * FF)] * 2 + [s(FF, D)] * 2
     outs += [s(4 * rows_of(u), full_shape(u)[1]) for u in range(6)]
-    outs += [s(T, D), s(D, T), s(T, D), s(T, D), s(D, T), s(T, FF), s(2 * STEPS, T, W, dtype=F32), s(T, FF), s(T, 2 * FF), s(T, FF), s(T, D), s(T, 2 * FF)]
+    outs += [s(T, D), s(D, T), s(T, D), s(T, D), s(D, T), s(T, FF), s(2 * STEPS, T, W, dtype=F32), s(T, 2 * FF), s(T, FF), s(T, D), s(T, 2 * FF)]
     scratch = [VMEM((2, D, FF), BF), VMEM((T, D), BF), VMEM((D, T), BF)]
     scratch += [VMEM((4, r, FF), BF) for r in (GROWS // 2, GROWS // 2, GROWS, GROWS)]
     scratch += [VMEM((2, r, D), BF) for r in (DROWS // 2, DROWS // 2, DROWS, DROWS)]

time: 414 us -> 415 us (level)
  no operation moved by 1% of the time
where the time goes in v5:
time: 415 us; the launch traced here: 414 us
  Pallas kernels  413 us (100%)
    pallas_call x2, Pallas kernels, body(): by_g, by_u, by_d, dx = hand_on(*step(x[0], dy[0], wg, wu, wd)[:4])  413 us

profile of v5, /device:TPU:0, one launch (start us, length us, event | category | flops | bytes accessed | tf_op | source)
XLA Modules:
  0.0 413.8 jit_solution(15636576345963432991)
XLA Ops:
  0.6 405.9 %step.1 = (bf16[2,128,2816]{2,1,0:T(8,128)(2,1)}, bf16[2,128,2816]{2,1,0:T(8,128)(2,1)}, bf16[2,352,1024]{2,1,0:T(8,128)(2,1)}, bf16[2048,1024]{1,0:T(8,128)(2,1...) custom-call(bf16[2048,1024]{1,0:T(8,128)(2,1)} %bitcast.3, ...), custom_call_target="tpu_custom_call" | custom-call | tf_op jit(solution)/shard_map/step/pallas_call | solution.py:568
  406.5 7.2 %hand_on.1 = (bf16[2,128,2816]{2,1,0:T(8,128)(2,1)}, bf16[2,128,2816]{2,1,0:T(8,128)(2,1)}, bf16[2,352,1024]{2,1,0:T(8,128)(2,1)}, bf16[2048,1024]{1,0:T(8,128)(2,1)}) custom-call(bf16[2,128,2816]{2,1,0:T(8,128)(2,1)} %get-tuple-element.12.refs_0_, bf16[2,128,2816]{2,1,0:T(8,128)(2,1)} %get-tuple-element.13.refs_1_, ...), custom_call_target="tpu_custom_call" | custom-call | tf_op jit(solution)/shard_map/hand_on/pallas_call | solution.py:568

commit v6 on v5

--- a/solution.py
+++ b/solution.py
@@ -488,13 +488,13 @@
     for u in range(6):
         for k in range(11):
             hop(u, k).wait_send()
-    grad_gu(1, 4, 5, dgu1, {3: fetch1(3), 4: pass1(3), 8: fetch2(3), 9: pass2(3)})
+    grad_gu(1, 4, 5, dgu1, {2: fetch1(3), 3: pass1(3), 7: (fetch2(3),), 8: pass2(3), 10: fetch1(4)})
     in_at = load(a0t, resident_t, 1)
     in_at.start()
     for c in in_w:
         c.wait()
-    grad_in(dgu1, h1, dy, dh1, True, {0: fetch1(4), 1: together(pass1(4), fetch1(5)), 2: pass1(5), 3: fetch2(4), 4: together(pass2(4), fetch3(3)), 5: together(pass3(3), fetch2(5)), 6: pass2(5)})
-    act_back(2, {3: fetch3(4), 4: pass3(4), 8: fetch3(5), 9: pass3(5)})
+    grad_in(dgu1, h1, dy, dh1, True, {0: pass1(4), 1: fetch3(3), 2: pass3(3), 3: fetch1(5), 4: together(pass1(5), fetch2(4)), 5: pass2(4)})
+    act_back(2, {2: fetch2(5), 3: pass2(5), 4: fetch3(4), 5: pass3(4), 8: fetch3(5), 9: pass3(5)})
     in_w = [load(full[i], weights.at[i], 2 + i) for i in range(2)]
     for c in in_w:
         c.start()
@@ -502,7 +502,9 @@
     grad_gu(0, 0, 1, dgu0, {2: fetch1(2), 3: pass1(2), 6: fetch2(2), 7: (pass2(2),), 10: fetch1(0)})
     for c in in_w:
         c.wait()
-    grad_in(dgu0, x, dh1, dx, False, {0: pass1(0), 1: fetch1(1), 2: together(pass1(1), fetch2(0)), 3: together(pass2(0), fetch3(2)), 4: pass3(2), 5: fetch2(1), 6: pass2(1), 7: fetch3(0)})
+    grad_in(dgu0, x, dh1, dx, False, {0: pass1(0), 1: fetch3(2), 2: together(pass3(2), fetch1(1)), 3: together(pass1(1), fetch2(0)), 4: pass2(0), 6: fetch2(1)})
+    pass2(1)()
+    fetch3(0)()
     pass3(0)()
     fetch3(1)()
     pass3(1)()

time: 415 us -> 404 us (0.973)
  Pallas kernels: 413 us -> 401 us
    pallas_call x2, Pallas kernels: 413 us -> 401 us  [body(): by_g, by_u, by_d, dx = hand_on(*step(x[0], dy[0], wg, wu, wd)[:4])]
where the time goes in v6:
time: 404 us; the launch traced here: 402 us
  Pallas kernels  401 us (99%)
    pallas_call x2, Pallas kernels, body(): by_g, by_u, by_d, dx = hand_on(*step(x[0], dy[0], wg, wu, wd)[:4])  401 us

profile of v6, /device:TPU:0, one launch (start us, length us, event | category | flops | bytes accessed | tf_op | source)
XLA Modules:
  0.0 402.0 jit_solution(7461415720985510387)
XLA Ops:
  0.6 394.1 %step.1 = (bf16[2,128,2816]{2,1,0:T(8,128)(2,1)}, bf16[2,128,2816]{2,1,0:T(8,128)(2,1)}, bf16[2,352,1024]{2,1,0:T(8,128)(2,1)}, bf16[2048,1024]{1,0:T(8,128)(2,1...) custom-call(bf16[2048,1024]{1,0:T(8,128)(2,1)} %bitcast.3, ...), custom_call_target="tpu_custom_call" | custom-call | tf_op jit(solution)/shard_map/step/pallas_call | solution.py:570
  394.7 7.2 %hand_on.1 = (bf16[2,128,2816]{2,1,0:T(8,128)(2,1)}, bf16[2,128,2816]{2,1,0:T(8,128)(2,1)}, bf16[2,352,1024]{2,1,0:T(8,128)(2,1)}, bf16[2048,1024]{1,0:T(8,128)(2,1)}) custom-call(bf16[2,128,2816]{2,1,0:T(8,128)(2,1)} %get-tuple-element.12.refs_0_, bf16[2,128,2816]{2,1,0:T(8,128)(2,1)} %get-tuple-element.13.refs_1_, ...), custom_call_target="tpu_custom_call" | custom-call | tf_op jit(solution)/shard_map/hand_on/pallas_call | solution.py:570

commit v7 on v6

--- a/solution.py
+++ b/solution.py
@@ -518,9 +518,9 @@
 
 def hand_on_kernel(*refs):
     sources, targets, buffers, sems = refs[:4], refs[4:8], refs[8:12], refs[12]
-    arrays = range(4)
-    ins = [pltpu.make_async_copy(sources[i], buffers[i], sems.at[i]) for i in arrays]
-    outs = [pltpu.make_async_copy(buffers[i], targets[i], sems.at[4 + i]) for i in arrays]
+    pieces = [(3, pl.ds(M * i, M)) for i in range(T // M)] + [(i, pl.ds(0, 2)) for i in range(3)]
+    ins = [pltpu.make_async_copy(sources[i].at[p], buffers[i].at[p], sems.at[0, n]) for n, (i, p) in enumerate(pieces)]
+    outs = [pltpu.make_async_copy(buffers[i].at[p], targets[i].at[p], sems.at[1, n]) for n, (i, p) in enumerate(pieces)]
     for c in ins:
         c.start()
     for c, o in zip(ins, outs):
@@ -562,7 +562,7 @@
         out_shape=outs[:4],
         in_specs=[any_] * 4,
         out_specs=[any_] * 4,
-        scratch_shapes=[VMEM(o.shape, BF) for o in outs[:4]] + [dma((8,))],
+        scratch_shapes=[VMEM(o.shape, BF) for o in outs[:4]] + [dma((2, 7))],
         name="hand_on",
     )
 

time: 404 us -> 403 us (level)
  no operation moved by 1% of the time
where the time goes in v7:
time: 403 us; the launch traced here: 402 us
  Pallas kernels  401 us (100%)
    pallas_call x2, Pallas kernels, body(): by_g, by_u, by_d, dx = hand_on(*step(x[0], dy[0], wg, wu, wd)[:4])  401 us

profile of v7, /device:TPU:0, one launch (start us, length us, event | category | flops | bytes accessed | tf_op | source)
XLA Modules:
  0.0 401.6 jit_solution(3720097300321018269)
XLA Ops:
  0.6 394.1 %step.1 = (bf16[2,128,2816]{2,1,0:T(8,128)(2,1)}, bf16[2,128,2816]{2,1,0:T(8,128)(2,1)}, bf16[2,352,1024]{2,1,0:T(8,128)(2,1)}, bf16[2048,1024]{1,0:T(8,128)(2,1...) custom-call(bf16[2048,1024]{1,0:T(8,128)(2,1)} %bitcast.3, ...), custom_call_target="tpu_custom_call" | custom-call | tf_op jit(solution)/shard_map/step/pallas_call | solution.py:570
  394.7 6.7 %hand_on.1 = (bf16[2,128,2816]{2,1,0:T(8,128)(2,1)}, bf16[2,128,2816]{2,1,0:T(8,128)(2,1)}, bf16[2,352,1024]{2,1,0:T(8,128)(2,1)}, bf16[2048,1024]{1,0:T(8,128)(2,1)}) custom-call(bf16[2,128,2816]{2,1,0:T(8,128)(2,1)} %get-tuple-element.12.refs_0_, bf16[2,128,2816]{2,1,0:T(8,128)(2,1)} %get-tuple-element.13.refs_1_, ...), custom_call_target="tpu_custom_call" | custom-call | tf_op jit(solution)/shard_map/hand_on/pallas_call | solution.py:570
